TPU v7x, 32 devices: a whole 2x2x4 slice. The times are simulated.
32 devices in a mesh: dp: 8 (over y, x, core), tensor: 4 (over z).
Axes of the slice: x: 2, y: 2, z: 4, core: 2. Of those that a mesh axis runs over, the one named last changes fastest.
Arguments:
- tokens: bfloat16 [32768, 768], P(('dp', 'tensor')), may hold values from -6 to 6
- cotangent: bfloat16 [32768, 768], P(('dp', 'tensor')), may hold values from -6 to 6
- lengths: int32 [32, 6], P('dp'), may hold values from 1 to 256, 1024 in all within a row
- drop_mask: int32 [2, 2, 32, 6], P(None, None, 'dp'), may hold values 0 or 1
- ln1_gain: float32 [2, 768], replicated, may hold values from 0.5 to 1.5
- ln1_bias: float32 [2, 768], replicated, may hold values from -1.25 to 1.25
- w_qkv: bfloat16 [2, 768, 3, 768], P(None, None, None, 'tensor'), may hold values from -0.21875 to 0.21875
- b_qv: bfloat16 [2, 2, 768], P(None, None, 'tensor'), may hold values from -1.75 to 1.75
- w_out: bfloat16 [2, 768, 768], P(None, 'tensor'), may hold values from -0.875 to 0.875
- b_out: bfloat16 [2, 768], replicated, may hold values from -1.75 to 1.75
- ln2_gain: float32 [2, 768], replicated, may hold values from 0.5 to 1.5
- ln2_bias: float32 [2, 768], replicated, may hold values from -1.25 to 1.25
- w_up: bfloat16 [2, 768, 3072], P(None, None, 'tensor'), may hold values from -0.21875 to 0.21875
- b_up: bfloat16 [2, 3072], P(None, 'tensor'), may hold values from -1.75 to 1.75
- w_down: bfloat16 [2, 3072, 768], P(None, 'tensor'), may hold values from -0.109375 to 0.109375
- b_down: bfloat16 [2, 768], replicated, may hold values from -1.75 to 1.75
Outputs:
- blocks_out: bfloat16 [2, 32768, 768], P(None, ('dp', 'tensor'))
- input_grad: float32 [32768, 768], P(('dp', 'tensor'))
- ln1_gain_grad: float32 [2, 768], replicated
- ln1_bias_grad: float32 [2, 768], replicated
- w_qkv_grad: float32 [2, 768, 3, 768], P(None, 'dp', None, 'tensor')
- b_qv_grad: float32 [2, 2, 768], replicated
- w_out_grad: float32 [2, 768, 768], P(None, 'tensor', 'dp')
- b_out_grad: float32 [2, 768], replicated
- ln2_gain_grad: float32 [2, 768], replicated
- ln2_bias_grad: float32 [2, 768], replicated
- w_up_grad: float32 [2, 768, 3072], P(None, 'dp', 'tensor')
- b_up_grad: float32 [2, 3072], replicated
- w_down_grad: float32 [2, 3072, 768], P(None, 'tensor', 'dp')
- b_down_grad: float32 [2, 768], replicated
Inputs may be any that keep to these rules, and one draw needn't show every extreme that they name: Each row's 6 lengths sum to 1024, and the largest in each row is 256.
All inputs are finite; a program needn't handle non-finite values. No bound on the sum of `drop_mask` on one device may be relied on, other than what follows from the above.
Results may differ from a plain program's by a relative error of at most 0.02.
Values may be sent and summed in bfloat16 or wider, within the bound.
A program may use at most 320 MiB of HBM per device.

v0:
```python
from functools import partial
import math

import jax
import jax.numpy as jnp
from jax import lax
from jax.sharding import PartitionSpec as P

HEAD_DIM = 64
FF = 3072
SEQ = 1024


eps_norm = 1e-06
survival = 0.9
masked_score = -1e30


def norm_forward(values, norm_gain, norm_shift):
    centre = values - jnp.mean(values, axis=-1, keepdims=True)
    spread = jnp.mean(centre * centre, axis=-1, keepdims=True)
    scaled = lax.rsqrt(spread + eps_norm)
    normalized = centre * scaled
    return (normalized * norm_gain + norm_shift, normalized, scaled)


def norm_backward(grad_out, normalized, scaled, norm_gain):
    grad_unit = grad_out * norm_gain
    inner = (
        grad_unit
        - jnp.mean(grad_unit, axis=-1, keepdims=True)
        - normalized * jnp.mean(grad_unit * normalized, axis=-1, keepdims=True)
    )
    return (inner * scaled, jnp.sum(grad_out * normalized, axis=0), jnp.sum(grad_out, axis=0))


def attend_scores(query_block, key_row, query_segment, key_segment, score_scale):
    scores = (
        jnp.einsum("qhd,khd->hqk", query_block, key_row, preferred_element_type=jnp.float32)
        * score_scale
    )
    same_segment = (query_segment[:, None] == key_segment[None, :])[None]
    return (jnp.where(same_segment, scores, masked_score), same_segment)


def attention_forward(queries, keys_all, values_all, segments, score_scale):
    row_length = queries.shape[1]
    block_rows = min(512, row_length)

    def one_row(row_item):
        query_row, key_row, value_row, segment_row = row_item
        mixed_parts = []
        total_parts = []
        for first_row in range(0, row_length, block_rows):
            last_row = first_row + block_rows
            scores, same_segment = attend_scores(
                query_row[first_row:last_row],
                key_row,
                segment_row[first_row:last_row],
                segment_row,
                score_scale,
            )
            row_top = jnp.max(scores, axis=-1, keepdims=True)
            exponent = jnp.exp(scores - row_top)
            row_total = jnp.sum(exponent, axis=-1, keepdims=True)
            weights_low = (exponent / row_total).astype(jnp.bfloat16)
            mixed_parts.append(
                jnp.einsum(
                    "hqk,khd->qhd", weights_low, value_row, preferred_element_type=jnp.float32
                )
            )
            total_parts.append(row_top + jnp.log(row_total))
        return (jnp.concatenate(mixed_parts, axis=0), jnp.concatenate(total_parts, axis=1))

    return lax.map(one_row, (queries, keys_all, values_all, segments))


def attention_backward(queries, keys_all, values_all, segments, grad_mixed, log_total, score_scale):
    row_length = queries.shape[1]
    block_rows = min(512, row_length)

    def one_row(row_item):
        query_row, key_row, value_row, segment_row, grad_row, total_row = row_item
        query_parts = []
        grad_keys = jnp.zeros(key_row.shape, jnp.float32)
        grad_values = jnp.zeros(value_row.shape, jnp.float32)
        for first_row in range(0, row_length, block_rows):
            last_row = first_row + block_rows
            query_block = query_row[first_row:last_row]
            grad_block = grad_row[first_row:last_row]
            scores, same_segment = attend_scores(
                query_block, key_row, segment_row[first_row:last_row], segment_row, score_scale
            )
            weights_soft = jnp.where(
                same_segment, jnp.exp(scores - total_row[:, first_row:last_row]), 0.0
            )
            grad_weights = jnp.einsum(
                "qhd,khd->hqk", grad_block, value_row, preferred_element_type=jnp.float32
            )
            grad_scores = (
                weights_soft
                * (grad_weights - jnp.sum(weights_soft * grad_weights, axis=-1, keepdims=True))
            ).astype(jnp.bfloat16)
            query_parts.append(
                jnp.einsum("hqk,khd->qhd", grad_scores, key_row, preferred_element_type=jnp.float32)
                * score_scale
            )
            grad_keys = (
                grad_keys
                + jnp.einsum(
                    "hqk,qhd->khd", grad_scores, query_block, preferred_element_type=jnp.float32
                )
                * score_scale
            )
            grad_values = grad_values + jnp.einsum(
                "hqk,qhd->khd",
                weights_soft.astype(jnp.bfloat16),
                grad_block,
                preferred_element_type=jnp.float32,
            )
        return (jnp.concatenate(query_parts, axis=0), grad_keys, grad_values)

    return lax.map(one_row, (queries, keys_all, values_all, segments, grad_mixed, log_total))


def per_device(
    tokens,
    cotangent,
    lengths,
    drop_mask,
    ln1_gain,
    ln1_bias,
    w_qkv,
    b_qv,
    w_out,
    b_out,
    ln2_gain,
    ln2_bias,
    w_up,
    b_up,
    w_down,
    b_down,
):
    layer_count = w_qkv.shape[0]
    local_rows, model_width = tokens.shape
    row_number, segment_count = lengths.shape
    tensor_index = lax.axis_index("tensor")
    score_scale = 1.0 / math.sqrt(HEAD_DIM)
    segment_ends = jnp.cumsum(lengths, axis=-1)
    positions = jnp.arange(SEQ, dtype=jnp.int32)
    segments = jnp.sum(
        (positions[None, :, None] >= segment_ends[:, None, :]).astype(jnp.int32), axis=-1
    )
    onehot = (
        segments[:, :, None] == jnp.arange(segment_count, dtype=jnp.int32)[None, None, :]
    ).astype(jnp.float32)
    keep_rows = (
        jnp.sum(onehot[None, None] * drop_mask.astype(jnp.float32)[:, :, :, None, :], axis=-1)
        / survival
    )
    keep_local = lax.dynamic_slice_in_dim(
        keep_rows.reshape(layer_count, 2, row_number * SEQ),
        tensor_index * local_rows,
        local_rows,
        2,
    )
    full_qkv, full_out, full_up, full_down, full_bqv, full_bup = (
        w_qkv,
        w_out,
        w_up,
        w_down,
        b_qv,
        b_up,
    )
    column_start = tensor_index * w_qkv.shape[3]
    hidden_start = tensor_index * w_up.shape[2]

    def move_norm_one(values):
        return lax.all_gather(values, "tensor", axis=0, tiled=True)

    def move_norm_two(values):
        return lax.all_gather(values, "tensor", axis=0, tiled=True)

    def sum_attn_out(partial_term):
        return lax.psum_scatter(
            partial_term(jnp.int32(0), lax.axis_size("tensor") * local_rows).astype(jnp.bfloat16),
            "tensor",
            scatter_dimension=0,
            tiled=True,
        ).astype(jnp.float32)

    def sum_mlp_out(partial_term):
        return lax.psum_scatter(
            partial_term(jnp.int32(0), local_rows * lax.axis_size("tensor")),
            "tensor",
            scatter_dimension=0,
            tiled=True,
        )

    head_cols = full_qkv.shape[3]
    head_count = head_cols // HEAD_DIM

    def layer_forward(hidden, layer_index, finish):
        normed_one, unit_one, scaled_one = norm_forward(
            hidden, ln1_gain[layer_index], ln1_bias[layer_index]
        )
        gathered_one = move_norm_one(normed_one.astype(jnp.bfloat16))
        group_rows = gathered_one.shape[0]
        work_count = group_rows // SEQ
        project = jnp.dot(
            gathered_one,
            full_qkv[layer_index].reshape(model_width, 3 * head_cols),
            preferred_element_type=jnp.float32,
        ).reshape(group_rows, 3, head_cols)
        bias_pair = full_bqv[layer_index].astype(jnp.float32)
        queries = (
            (project[:, 0] + bias_pair[0])
            .astype(jnp.bfloat16)
            .reshape(work_count, SEQ, head_count, HEAD_DIM)
        )
        keys_all = project[:, 1].astype(jnp.bfloat16).reshape(work_count, SEQ, head_count, HEAD_DIM)
        values_all = (
            (project[:, 2] + bias_pair[1])
            .astype(jnp.bfloat16)
            .reshape(work_count, SEQ, head_count, HEAD_DIM)
        )
        mixed_out, log_total = attention_forward(
            queries, keys_all, values_all, segments, score_scale
        )
        mixed_low = mixed_out.reshape(group_rows, head_cols).astype(jnp.bfloat16)
        weight_out = full_out[layer_index]

        def out_term(first_row, count_rows):
            return jnp.dot(
                lax.dynamic_slice_in_dim(mixed_low, first_row, count_rows, 0),
                weight_out,
                preferred_element_type=jnp.float32,
            )

        attn_sum = sum_attn_out(out_term)
        middle = hidden + keep_local[layer_index, 0][:, None] * (
            attn_sum + b_out[layer_index].astype(jnp.float32)
        )
        normed_two, unit_two, scaled_two = norm_forward(
            middle, ln2_gain[layer_index], ln2_bias[layer_index]
        )
        gathered_two = move_norm_two(normed_two.astype(jnp.bfloat16))
        upward = jnp.dot(
            gathered_two, full_up[layer_index], preferred_element_type=jnp.float32
        ) + full_bup[layer_index].astype(jnp.float32)
        active = jax.nn.gelu(upward, approximate=False).astype(jnp.bfloat16)
        kept_state = (
            unit_one,
            scaled_one,
            gathered_one,
            queries,
            keys_all,
            values_all,
            log_total,
            mixed_low,
            unit_two,
            scaled_two,
            gathered_two,
            upward,
            active,
        )
        if not finish:
            return (middle, kept_state)
        weight_down = full_down[layer_index]

        def down_term(first_row, count_rows):
            return jnp.dot(
                lax.dynamic_slice_in_dim(active, first_row, count_rows, 0),
                weight_down,
                preferred_element_type=jnp.float32,
            )

        down_sum = sum_mlp_out(down_term)
        produced = middle + keep_local[layer_index, 1][:, None] * (
            down_sum + b_down[layer_index].astype(jnp.float32)
        )
        return (produced, kept_state)

    inputs = [tokens.astype(jnp.float32)]
    for layer_index in range(layer_count):
        produced, unused = layer_forward(inputs[-1], layer_index, True)
        inputs.append(produced)
    blocks_out = jnp.stack(inputs[1:]).astype(jnp.bfloat16)
    grad_flow = cotangent.astype(jnp.float32)
    collected = []
    for layer_index in reversed(range(layer_count)):
        middle, kept_state = layer_forward(inputs[layer_index], layer_index, False)
        (
            unit_one,
            scaled_one,
            gathered_one,
            queries,
            keys_all,
            values_all,
            log_total,
            mixed_low,
            unit_two,
            scaled_two,
            gathered_two,
            upward,
            active,
        ) = kept_state
        group_rows = gathered_one.shape[0]
        work_count = group_rows // SEQ
        branch_two = keep_local[layer_index, 1][:, None] * grad_flow
        grad_bias_down = jnp.sum(branch_two, axis=0)
        gathered_grad_two = lax.all_gather(
            branch_two.astype(jnp.bfloat16), "tensor", axis=0, tiled=True
        )
        grad_weight_down = jnp.einsum(
            "tf,td->fd", active, gathered_grad_two, preferred_element_type=jnp.float32
        )
        grad_active = jnp.einsum(
            "td,fd->tf",
            gathered_grad_two,
            full_down[layer_index],
            preferred_element_type=jnp.float32,
        )
        unused, gelu_pull = jax.vjp(partial(jax.nn.gelu, approximate=False), upward)
        grad_upward = gelu_pull(grad_active)[0]
        grad_bias_up = jnp.sum(grad_upward, axis=0)
        upward_low = grad_upward.astype(jnp.bfloat16)
        grad_weight_up = jnp.einsum(
            "td,tf->df", gathered_two, upward_low, preferred_element_type=jnp.float32
        )
        weight_up = full_up[layer_index]
        grad_normed_two = lax.psum_scatter(
            jnp.einsum(
                "tf,df->td",
                lax.dynamic_slice_in_dim(
                    upward_low, jnp.int32(0), lax.axis_size("tensor") * local_rows, 0
                ),
                weight_up,
                preferred_element_type=jnp.float32,
            ).astype(jnp.bfloat16),
            "tensor",
            scatter_dimension=0,
            tiled=True,
        ).astype(jnp.float32)
        grad_part, grad_gain_two, grad_shift_two = norm_backward(
            grad_normed_two, unit_two, scaled_two, ln2_gain[layer_index]
        )
        grad_middle = grad_flow + grad_part
        branch_one = keep_local[layer_index, 0][:, None] * grad_middle
        grad_bias_out = jnp.sum(branch_one, axis=0)
        gathered_grad_one = lax.all_gather(
            branch_one.astype(jnp.bfloat16), "tensor", axis=0, tiled=True
        )
        grad_weight_out = jnp.einsum(
            "tc,td->cd", mixed_low, gathered_grad_one, preferred_element_type=jnp.float32
        )
        grad_mixed = jnp.einsum(
            "td,cd->tc",
            gathered_grad_one,
            full_out[layer_index],
            preferred_element_type=jnp.float32,
        )
        grad_mixed = grad_mixed.astype(jnp.bfloat16).reshape(work_count, SEQ, head_count, HEAD_DIM)
        grad_queries, grad_keys, grad_values = attention_backward(
            queries, keys_all, values_all, segments, grad_mixed, log_total, score_scale
        )
        grad_queries = grad_queries.reshape(group_rows, head_cols)
        grad_keys = grad_keys.reshape(group_rows, head_cols)
        grad_values = grad_values.reshape(group_rows, head_cols)
        grad_bias_qv = jnp.stack([jnp.sum(grad_queries, axis=0), jnp.sum(grad_values, axis=0)])
        grad_project = (
            jnp.stack([grad_queries, grad_keys, grad_values], axis=1)
            .reshape(group_rows, 3 * head_cols)
            .astype(jnp.bfloat16)
        )
        grad_weight_qkv = jnp.einsum(
            "td,tc->dc", gathered_one, grad_project, preferred_element_type=jnp.float32
        ).reshape(model_width, 3, head_cols)
        weight_flat = full_qkv[layer_index].reshape(model_width, 3 * head_cols)
        grad_normed_one = lax.psum_scatter(
            jnp.einsum(
                "tc,dc->td",
                lax.dynamic_slice_in_dim(
                    grad_project, jnp.int32(0), lax.axis_size("tensor") * local_rows, 0
                ),
                weight_flat,
                preferred_element_type=jnp.float32,
            ).astype(jnp.bfloat16),
            "tensor",
            scatter_dimension=0,
            tiled=True,
        ).astype(jnp.float32)
        grad_part, grad_gain_one, grad_shift_one = norm_backward(
            grad_normed_one, unit_one, scaled_one, ln1_gain[layer_index]
        )
        grad_flow = grad_middle + grad_part
        collected.append(
            (
                grad_gain_one,
                grad_shift_one,
                grad_weight_qkv,
                grad_bias_qv,
                grad_weight_out,
                grad_bias_out,
                grad_gain_two,
                grad_shift_two,
                grad_weight_up,
                grad_bias_up,
                grad_weight_down,
                grad_bias_down,
            )
        )
    collected = collected[::-1]

    def stack_field(position):
        return jnp.stack([layer_entry[position] for layer_entry in collected])

    padded_qv = lax.dynamic_update_slice(
        jnp.zeros((layer_count, 2, model_width), jnp.float32), stack_field(3), (0, 0, column_start)
    )
    padded_up = lax.dynamic_update_slice(
        jnp.zeros((layer_count, FF), jnp.float32), stack_field(9), (0, hidden_start)
    )
    reduced_small = lax.psum(
        (
            stack_field(0),
            stack_field(1),
            padded_qv,
            stack_field(5),
            stack_field(6),
            stack_field(7),
            padded_up,
            stack_field(11),
        ),
        ("dp", "tensor"),
    )
    reduced_large = (stack_field(2), stack_field(4), stack_field(8), stack_field(10))
    reduced_large = (
        lax.psum_scatter(reduced_large[0], "dp", scatter_dimension=1, tiled=True),
        lax.psum_scatter(reduced_large[1], "dp", scatter_dimension=2, tiled=True),
        lax.psum_scatter(reduced_large[2], "dp", scatter_dimension=1, tiled=True),
        lax.psum_scatter(reduced_large[3], "dp", scatter_dimension=2, tiled=True),
    )
    return (
        blocks_out,
        grad_flow,
        reduced_small[0],
        reduced_small[1],
        reduced_large[0],
        reduced_small[2],
        reduced_large[1],
        reduced_small[3],
        reduced_small[4],
        reduced_small[5],
        reduced_large[2],
        reduced_small[6],
        reduced_large[3],
        reduced_small[7],
    )


def solution(mesh):
    in_specs = (
        P(("dp", "tensor"), None),
        P(("dp", "tensor"), None),
        P("dp", None),
        P(None, None, "dp", None),
        P(),
        P(),
        P(None, None, None, "tensor"),
        P(None, None, "tensor"),
        P(None, "tensor", None),
        P(),
        P(),
        P(),
        P(None, None, "tensor"),
        P(None, "tensor"),
        P(None, "tensor", None),
        P(),
    )
    out_specs = (
        P(None, ("dp", "tensor"), None),
        P(("dp", "tensor"), None),
        P(),
        P(),
        P(None, "dp", None, "tensor"),
        P(),
        P(None, "tensor", "dp"),
        P(),
        P(),
        P(),
        P(None, "dp", "tensor"),
        P(),
        P(None, "tensor", "dp"),
        P(),
    )
    return jax.shard_map(
        per_device, mesh=mesh, in_specs=in_specs, out_specs=out_specs, check_vma=False
    )
```

profile of v0, /device:TPU:8, one launch (start us, length us, event | category | flops | bytes accessed | tf_op | source)
XLA Modules:
  0.0 3595.1 jit_solution(8966958518976299921)
XLA Ops:
  18.0 111.9 %all-gather.11.cloned.1.call-done = bf16[4096,768]{1,0:T(8,128)(2,1)} async-done(((bf16[1024,768]{1,0:T(8,128)(2,1)}), bf16[4096,768]{1,0:T(8,128)(2,1)}) %all-gather.11.cloned.1.call-update) | async-done | bytes 6291472 | tf_op jit(solution)/shard_map/all_gather | solution.py:179
  159.3 89.1 %while.72 = (s32[]{:T(128)}, bf16[4,1024,3,64]{1,3,2,0:T(8,128)(2,1)S(1)}, bf16[4,1024,3,64]{1,3,2,0:T(8,128)(2,1)}, s32[4,1024]{1,0:T(4,128)S(1)}, bf16[4,1024,...) while((s32[]{:T(128)}, ...), condition=%wide.region_10.11_spmd, body=%wide.region_5.10_spmd.sunk | while | flops 826017792 | bytes 30460552 | solution.py:75
  256.1 62.3 %while.76 = (s32[]{:T(128)}, bf16[4,1024,3,64]{1,3,2,0:T(8,128)(2,1)S(1)}, f32[4,3,1024,1]{2,1,3,0:T(4,128)S(1)}, bf16[4,1024,3,64]{1,3,2,0:T(8,128)(2,1)}, s32[...) while((s32[]{:T(128)}, ...), condition=%wide.region_51.52_spmd, body=%wide.region_46.51_spmd.sunk | while | flops 844890112 | bytes 45247124 | solution.py:75
  329.1 37.7 %reduce-scatter.18.cloned.1.call-done = bf16[1024,768]{1,0:T(8,128)(2,1)} async-done(((bf16[4096,768]{1,0:T(8,128)(2,1)}), bf16[1024,768]{1,0:T(8,128)(2,1)}) %reduce-scatter.18.cloned.1.call-update) | async-done | bytes 1572880 | tf_op jit(solution)/shard_map/reduce_scatter | solution.py:185
  366.8 113.6 %reduce-scatter.32.cloned.1.call-done = bf16[1024,768]{1,0:T(8,128)(2,1)} async-done(((bf16[4096,768]{1,0:T(8,128)(2,1)}), bf16[1024,768]{1,0:T(8,128)(2,1)}) %reduce-scatter.32.cloned.1.call-update) | async-done | bytes 1572880 | tf_op jit(solution)/shard_map/reduce_scatter | solution.py:185
  490.9 112.3 %all-gather.13.cloned.1.call-done = bf16[4096,768]{1,0:T(8,128)(2,1)} async-done(((bf16[1024,768]{1,0:T(8,128)(2,1)}), bf16[4096,768]{1,0:T(8,128)(2,1)}) %all-gather.13.cloned.1.call-update) | async-done | bytes 6291472 | tf_op jit(solution)/shard_map/all_gather | solution.py:182
  603.2 41.0 %fusion.310 = f32[4096,768]{1,0:T(8,128)} fusion(f32[768]{0:T(1024)S(1)} %get-tuple-element.548, bf16[4096,768]{1,0:T(8,128)(2,1)} %all-gather.13.cloned.1.call-done, bf16[2,768,768]{2,1,0:T(8,128)(2,1)} %param.42, bf16[2,768,768]{2,1,0:T(8,128)(2,1)} %param.40), kind=kOutput, calls=%fused_computation.410 | convolution fusion | flops 9871294464 | bytes 21236736 | tf_op jit(solution)/shard_map/dot_general | solution.py:272
  645.5 211.9 %reduce-scatter.20.cloned.1.call-done = f32[1024,768]{1,0:T(8,128)} async-done(((f32[4096,768]{1,0:T(8,128)}), f32[1024,768]{1,0:T(8,128)}) %reduce-scatter.20.cloned.1.call-update) | async-done | bytes 3145744 | tf_op jit(solution)/shard_map/reduce_scatter | solution.py:193
  866.0 113.3 %all-gather.15.cloned.1.call-done = bf16[4096,768]{1,0:T(8,128)(2,1)} async-done(((bf16[1024,768]{1,0:T(8,128)(2,1)}), bf16[4096,768]{1,0:T(8,128)(2,1)}) %all-gather.15.cloned.1.call-update) | async-done | bytes 6291472 | tf_op jit(solution)/shard_map/all_gather | solution.py:179
  1008.5 88.2 %while.73 = (s32[]{:T(128)}, bf16[4,1024,3,64]{1,3,2,0:T(8,128)(2,1)S(1)}, bf16[4,1024,3,64]{1,3,2,0:T(8,128)(2,1)}, s32[4,1024]{1,0:T(4,128)S(1)}, bf16[4,1024,...) while((s32[]{:T(128)}, ...), condition=%wide.region_22.23_spmd, body=%wide.region_17.22_spmd.sunk | while | flops 826017792 | bytes 30460552 | solution.py:75
  1104.4 62.6 %while.74 = (s32[]{:T(128)}, bf16[4,1024,3,64]{1,3,2,0:T(8,128)(2,1)S(1)}, f32[4,3,1024,1]{2,1,3,0:T(4,128)S(1)}, bf16[4,1024,3,64]{1,3,2,0:T(8,128)(2,1)}, s32[...) while((s32[]{:T(128)}, ...), condition=%wide.region_32.33_spmd, body=%wide.region_27.32_spmd.sunk | while | flops 844890112 | bytes 45247124 | solution.py:75
  1174.6 40.5 %reduce-scatter.22.cloned.1.call-done = bf16[1024,768]{1,0:T(8,128)(2,1)} async-done(((bf16[4096,768]{1,0:T(8,128)(2,1)}), bf16[1024,768]{1,0:T(8,128)(2,1)}) %reduce-scatter.22.cloned.1.call-update) | async-done | bytes 1572880 | tf_op jit(solution)/shard_map/reduce_scatter | solution.py:185
  1215.1 113.6 %reduce-scatter.26.cloned.1.call-done = bf16[1024,768]{1,0:T(8,128)(2,1)} async-done(((bf16[4096,768]{1,0:T(8,128)(2,1)}), bf16[1024,768]{1,0:T(8,128)(2,1)}) %reduce-scatter.26.cloned.1.call-update) | async-done | bytes 1572880 | tf_op jit(solution)/shard_map/reduce_scatter | solution.py:185
  1338.3 110.5 %all-gather.19.cloned.1.call-done = bf16[4096,768]{1,0:T(8,128)(2,1)} async-done(((bf16[1024,768]{1,0:T(8,128)(2,1)}), bf16[4096,768]{1,0:T(8,128)(2,1)}) %all-gather.19.cloned.1.call-update) | async-done | bytes 6291472 | tf_op jit(solution)/shard_map/all_gather | solution.py:182
  1448.9 33.5 fusion.266
  1482.4 81.4 %all-gather.21.cloned.1.call-done = bf16[4096,768]{1,0:T(8,128)(2,1)} async-done(((bf16[1024,768]{1,0:T(8,128)(2,1)}), bf16[4096,768]{1,0:T(8,128)(2,1)}) %all-gather.21.cloned.1.call-update) | async-done | bytes 6291472 | tf_op jit(solution)/shard_map/all_gather | solution.py:312
  1592.9 112.0 %reduce-scatter.28.cloned.1.call-done = bf16[1024,768]{1,0:T(8,128)(2,1)} async-done(((bf16[4096,768]{1,0:T(8,128)(2,1)}), bf16[1024,768]{1,0:T(8,128)(2,1)}) %reduce-scatter.28.cloned.1.call-update) | async-done | bytes 1572880 | tf_op jit(solution)/shard_map/reduce_scatter | solution.py:332
  1714.8 109.7 %all-gather.23.cloned.1.call-done = bf16[4096,768]{1,0:T(8,128)(2,1)} async-done(((bf16[1024,768]{1,0:T(8,128)(2,1)}), bf16[4096,768]{1,0:T(8,128)(2,1)}) %all-gather.23.cloned.1.call-update) | async-done | bytes 6291472 | tf_op jit(solution)/shard_map/all_gather | solution.py:351
  1838.1 144.9 %while.75 = (s32[]{:T(128)}, f32[4,1024,3,64]{1,3,2,0:T(8,128)}, bf16[4,1024,3,64]{1,0,3,2:T(4,128)(2,1)}, f32[4,1024,3,64]{1,3,2,0:T(8,128)}, bf16[4,1024,3,64]...) while((s32[]{:T(128)}, f32[4,1024,3,64]{1,3,2,0:T(8,128)}, ...), condition=%wide.region_42.43_spmd, body=%wide.region_39.42_spmd.sunk | while | flops 2046948352 | bytes 152817968 | solution.py:123
  2012.4 111.5 %reduce-scatter.30.cloned.1.call-done = bf16[1024,768]{1,0:T(8,128)(2,1)} async-done(((bf16[4096,768]{1,0:T(8,128)(2,1)}), bf16[1024,768]{1,0:T(8,128)(2,1)}) %reduce-scatter.30.cloned.1.call-update) | async-done | bytes 1572880 | tf_op jit(solution)/shard_map/reduce_scatter | solution.py:380
  2131.3 113.0 %all-gather.17.cloned.1.call-done = bf16[4096,768]{1,0:T(8,128)(2,1)} async-done(((bf16[1024,768]{1,0:T(8,128)(2,1)}), bf16[4096,768]{1,0:T(8,128)(2,1)}) %all-gather.17.cloned.1.call-update) | async-done | bytes 6291472 | tf_op jit(solution)/shard_map/all_gather | solution.py:182
  2244.3 41.1 %fusion.306 = f32[4096,768]{1,0:T(8,128)} fusion(f32[768]{0:T(1024)S(1)} %copy-done.134, bf16[4096,768]{1,0:T(8,128)(2,1)} %all-gather.17.cloned.1.call-done, bf16[2,768,768]{2,1,0:T(8,128)(2,1)} %param.42, bf16[2,768,768]{2,1,0:T(8,128)(2,1)} %param.40), kind=kOutput, calls=%fused_computation.408 | convolution fusion | flops 9871294464 | bytes 21236736 | tf_op jit(solution)/shard_map/dot_general | solution.py:272
  2286.2 212.5 %reduce-scatter.24.cloned.1.call-done = f32[1024,768]{1,0:T(8,128)} async-done(((f32[4096,768]{1,0:T(8,128)}), f32[1024,768]{1,0:T(8,128)}) %reduce-scatter.24.cloned.1.call-update) | async-done | bytes 3145744 | tf_op jit(solution)/shard_map/reduce_scatter | solution.py:193
  2508.9 104.6 %all-gather.25.cloned.1.call-done = bf16[4096,768]{1,0:T(8,128)(2,1)} async-done(((bf16[1024,768]{1,0:T(8,128)(2,1)}), bf16[4096,768]{1,0:T(8,128)(2,1)}) %all-gather.25.cloned.1.call-update) | async-done | bytes 6291472 | tf_op jit(solution)/shard_map/all_gather | solution.py:182
  2613.5 33.5 fusion.267
  2647.1 82.0 %all-gather.27.cloned.1.call-done = bf16[4096,768]{1,0:T(8,128)(2,1)} async-done(((bf16[1024,768]{1,0:T(8,128)(2,1)}), bf16[4096,768]{1,0:T(8,128)(2,1)}) %all-gather.27.cloned.1.call-update) | async-done | bytes 6291472 | tf_op jit(solution)/shard_map/all_gather | solution.py:312
  2757.2 112.0 %reduce-scatter.34.cloned.1.call-done = bf16[1024,768]{1,0:T(8,128)(2,1)} async-done(((bf16[4096,768]{1,0:T(8,128)(2,1)}), bf16[1024,768]{1,0:T(8,128)(2,1)}) %reduce-scatter.34.cloned.1.call-update) | async-done | bytes 1572880 | tf_op jit(solution)/shard_map/reduce_scatter | solution.py:332
  2929.3 63.2 %all-gather.29.cloned.1.call-done = bf16[4096,768]{1,0:T(8,128)(2,1)} async-done(((bf16[1024,768]{1,0:T(8,128)(2,1)}), bf16[4096,768]{1,0:T(8,128)(2,1)}) %all-gather.29.cloned.1.call-update) | async-done | bytes 6291472 | tf_op jit(solution)/shard_map/all_gather | solution.py:351
  3006.0 146.2 %while.77 = (s32[]{:T(128)}, f32[4,1024,3,64]{1,3,2,0:T(8,128)}, bf16[4,1024,3,64]{1,0,3,2:T(4,128)(2,1)}, f32[4,1024,3,64]{1,3,2,0:T(8,128)}, bf16[4,1024,3,64]...) while((s32[]{:T(128)}, f32[4,1024,3,64]{1,3,2,0:T(8,128)}, ...), condition=%wide.region_61.62_spmd, body=%wide.region_58.61_spmd.sunk | while | flops 2046948352 | bytes 152817968 | solution.py:123
  3275.3 110.6 %reduce-scatter.36.cloned.1.call-done = bf16[1024,768]{1,0:T(8,128)(2,1)} async-done(((bf16[4096,768]{1,0:T(8,128)(2,1)}), bf16[1024,768]{1,0:T(8,128)(2,1)}) %reduce-scatter.36.cloned.1.call-update) | async-done | bytes 1572880 | tf_op jit(solution)/shard_map/reduce_scatter | solution.py:380
  3394.1 49.9 %reduce-scatter.38.cloned.1.call-done = f32[2,96,768]{2,1,0:T(8,128)} async-done(((f32[2,768,768]{2,1,0:T(8,128)}), f32[2,96,768]{2,1,0:T(8,128)}) %reduce-scatter.38.cloned.1.call-update) | async-done | bytes 589840 | tf_op jit(solution)/shard_map/reduce_scatter | solution.py:441
  3444.0 134.0 %all-reduce.7.cloned.1.call-done = (f32[2,768]{1,0:T(2,128)}, f32[2,768]{1,0:T(2,128)}, f32[2,2,768]{2,1,0:T(2,128)}, f32[2,768]{1,0:T(2,128)}, f32[2,768]{1,0:T...) async-done(((f32[2,768]{1,0:T(2,128)}, f32[2,768]{1,0:T(2,128)}, f32[2,2,768]{2,1,0:T(2,128)}, f32[2,768]{1,0:T(2,128)}, f32[2,768]{1,0:T(2,128)}, ...) | async-done | bytes 73744 | tf_op jit(solution)/shard_map/psum | solution.py:424
  (916 shorter events, 1063.5 us)
Async XLA Ops:
  7.2 122.7 %all-gather.11.cloned.1.call-start = ((), (), s32[]{:S(2)}) async-start(), calls=%async_computation.13 | async-start | bytes 7864320 | tf_op jit(solution)/shard_map/all_gather | solution.py:179
  16.2 350.7 %reduce-scatter.18.cloned.1.call-start = ((), (), s32[]{:S(2)}) async-start(), calls=%async_computation.14 | async-start | bytes 7864320 | tf_op jit(solution)/shard_map/reduce_scatter | solution.py:185
  254.8 225.7 %reduce-scatter.32.cloned.1.call-start = ((), (), s32[]{:S(2)}) async-start(), calls=%async_computation.27 | async-start | bytes 7864320 | tf_op jit(solution)/shard_map/reduce_scatter | solution.py:185
  326.1 277.1 %all-gather.13.cloned.1.call-start = ((), (), s32[]{:S(2)}) async-start(), calls=%async_computation.15 | async-start | bytes 7864320 | tf_op jit(solution)/shard_map/all_gather | solution.py:182
  490.2 367.2 %reduce-scatter.20.cloned.1.call-start = ((), (), s32[]{:S(2)}) async-start(), calls=%async_computation.16 | async-start | bytes 15728640 | tf_op jit(solution)/shard_map/reduce_scatter | solution.py:193
  644.3 335.1 %all-gather.15.cloned.1.call-start = ((), (), s32[]{:S(2)}) async-start(), calls=%async_computation.17 | async-start | bytes 7864320 | tf_op jit(solution)/shard_map/all_gather | solution.py:179
  865.7 349.4 %reduce-scatter.22.cloned.1.call-start = ((), (), s32[]{:S(2)}) async-start(), calls=%async_computation.18 | async-start | bytes 7864320 | tf_op jit(solution)/shard_map/reduce_scatter | solution.py:185
  1103.0 225.7 %reduce-scatter.26.cloned.1.call-start = ((), (), s32[]{:S(2)}) async-start(), calls=%async_computation.21 | async-start | bytes 7864320 | tf_op jit(solution)/shard_map/reduce_scatter | solution.py:185
  1174.6 274.3 %all-gather.19.cloned.1.call-start = ((), (), s32[]{:S(2)}) async-start(), calls=%async_computation.22 | async-start | bytes 7864320 | tf_op jit(solution)/shard_map/all_gather | solution.py:182
  1335.8 228.0 %all-gather.21.cloned.1.call-start = ((), (), s32[]{:S(2)}) async-start(), calls=%async_computation.23 | async-start | bytes 7864320 | tf_op jit(solution)/shard_map/all_gather | solution.py:312
  1338.1 366.9 %reduce-scatter.28.cloned.1.call-start = ((), (), s32[]{:S(2)}) async-start(), calls=%async_computation.24 | async-start | bytes 7864320 | tf_op jit(solution)/shard_map/reduce_scatter | solution.py:332
  1592.9 231.7 %all-gather.23.cloned.1.call-start = ((), (), s32[]{:S(2)}) async-start(), calls=%async_computation.25 | async-start | bytes 7864320 | tf_op jit(solution)/shard_map/all_gather | solution.py:351
  1711.5 412.3 %reduce-scatter.30.cloned.1.call-start = ((), (), s32[]{:S(2)}) async-start(), calls=%async_computation.26 | async-start | bytes 7864320 | tf_op jit(solution)/shard_map/reduce_scatter | solution.py:380
  2011.8 232.5 %all-gather.17.cloned.1.call-start = ((), (), s32[]{:S(2)}) async-start(), calls=%async_computation.19 | async-start | bytes 7864320 | tf_op jit(solution)/shard_map/all_gather | solution.py:182
  2131.2 367.4 %reduce-scatter.24.cloned.1.call-start = ((), (), s32[]{:S(2)}) async-start(), calls=%async_computation.20 | async-start | bytes 15728640 | tf_op jit(solution)/shard_map/reduce_scatter | solution.py:193
  2285.4 213.3 %copy-start.5 = (f32[1024,768]{1,0:T(8,128)S(1)}, f32[1024,768]{1,0:T(8,128)}, u32[]{:S(2)}) copy-start(f32[1024,768]{1,0:T(8,128)} %copy-done.2) | copy-start | bytes 9437188
  2285.4 213.3 %copy-start.75 = (f32[1,1,1024]{2,1,0:T(1,128)S(1)}, f32[1,1,1024]{2,1,0:T(1,128)}, u32[]{:S(2)}) copy-start(f32[1,1,1024]{2,1,0:T(1,128)} %get-tuple-element.737) | copy-start | bytes 12292
  2285.4 213.3 %copy-start.80 = (f32[768]{0:T(1024)S(1)}, f32[768]{0:T(1024)}, u32[]{:S(2)}) copy-start(f32[768]{0:T(1024)} %get-tuple-element.546) | copy-start | bytes 9220
  2285.4 213.3 %copy-start.83 = (f32[1024]{0:T(1024)S(1)}, f32[1024]{0:T(1024)}, u32[]{:S(2)}) copy-start(f32[1024]{0:T(1024)} %copy-done.81) | copy-start | bytes 12292
  2285.4 213.3 %copy-start.93 = (f32[768]{0:T(1024)S(1)}, f32[768]{0:T(1024)}, u32[]{:S(2)}) copy-start(f32[768]{0:T(1024)} %get-tuple-element.751) | copy-start | bytes 9220
  2285.4 213.3 %copy-start.98 = (f32[1024]{0:T(1024)S(1)}, f32[1024]{0:T(1024)}, u32[]{:S(2)}) copy-start(f32[1024]{0:T(1024)} %copy-done.96) | copy-start | bytes 12292
  2285.5 328.0 %all-gather.25.cloned.1.call-start = ((), (), s32[]{:S(2)}) async-start(), calls=%async_computation.28 | async-start | bytes 7864320 | tf_op jit(solution)/shard_map/all_gather | solution.py:182
  2286.1 443.0 %all-gather.27.cloned.1.call-start = ((), (), s32[]{:S(2)}) async-start(), calls=%async_computation.29 | async-start | bytes 7864320 | tf_op jit(solution)/shard_map/all_gather | solution.py:312
  2508.8 220.3 %copy-start.142 = (bf16[2,768,768]{2,1,0:T(8,128)(2,1)S(1)}, bf16[2,768,768]{2,1,0:T(8,128)(2,1)}, u32[]{:S(2)}) copy-start(bf16[2,768,768]{2,1,0:T(8,128)(2,1)} %param.42) | copy-start | bytes 7077892
  2508.8 360.4 %reduce-scatter.34.cloned.1.call-start = ((), (), s32[]{:S(2)}) async-start(), calls=%async_computation.30 | async-start | bytes 7864320 | tf_op jit(solution)/shard_map/reduce_scatter | solution.py:332
  2757.2 235.4 %all-gather.29.cloned.1.call-start = ((), (), s32[]{:S(2)}) async-start(), calls=%async_computation.31 | async-start | bytes 7864320 | tf_op jit(solution)/shard_map/all_gather | solution.py:351
  2879.5 366.5 %all-reduce.5.cloned.1.call-start = ((), (), s32[]{:S(2)}) async-start(), calls=%async_computation.36 | async-start | bytes 9437184
  2929.2 325.9 %reduce-scatter.42.cloned.1.call-start = ((), (), s32[]{:S(2)}) async-start(), calls=%async_computation.35 | async-start | bytes 1327104
  3183.2 89.5 %reduce-scatter.40.cloned.1.call-start = ((), (), s32[]{:S(2)}) async-start(), calls=%async_computation.34 | async-start | bytes 3981312
  3206.2 179.6 %reduce-scatter.36.cloned.1.call-start = ((), (), s32[]{:S(2)}) async-start(), calls=%async_computation.32 | async-start | bytes 7864320 | tf_op jit(solution)/shard_map/reduce_scatter | solution.py:380
  3216.0 228.0 %reduce-scatter.38.cloned.1.call-start = ((), (), s32[]{:S(2)}) async-start(), calls=%async_computation.33 | async-start | bytes 5308416 | tf_op jit(solution)/shard_map/reduce_scatter | solution.py:441
  3236.8 341.2 %all-reduce.7.cloned.1.call-start = ((), (), s32[]{:S(2)}) async-start(), calls=%async_computation.37 | async-start | bytes 147456 | tf_op jit(solution)/shard_map/psum | solution.py:424
  (165 other events, 6148.4 us)
Sparse Core Ops, SparseCore 0:
  16.3 113.5 all-gather.10
  254.9 111.9 reduce-scatter.17
  369.2 111.2 reduce-scatter.31
  490.3 112.8 all-gather.12
  644.4 213.0 reduce-scatter.19
  865.9 113.3 all-gather.14
  1103.1 111.9 reduce-scatter.21
  1217.4 111.2 reduce-scatter.25
  1335.9 112.8 all-gather.18
  1450.3 113.5 all-gather.20
  1593.0 111.9 reduce-scatter.27
  1711.7 112.8 all-gather.22
  2011.9 111.9 reduce-scatter.29
  2131.4 112.8 all-gather.16
  2285.6 213.0 reduce-scatter.23
  2500.1 113.3 all-gather.24
  2615.5 113.5 all-gather.26
  2757.3 111.9 reduce-scatter.33
  2879.6 112.8 all-gather.28
  2995.7 87.7 all-reduce.4
  3183.3 37.8 reduce-scatter.41
  3224.8 47.9 reduce-scatter.39
  3275.0 110.7 reduce-scatter.35
  3389.7 54.2 reduce-scatter.37
  3451.6 126.4 all-reduce.6
where the time goes:
time: 3610 us; the launch traced here: 3600 us
  waiting for transfers between devices  2380 us (66%)
  matrix products  767 us (21%)
  local copies, waits for them, and re-layouts  218 us (6%)
  other arithmetic  209 us (6%)
    all_gather x4, waiting for transfers between devices, move_norm_two(): return lax.all_gather(values, 'tensor', axis=0, tiled=True)  440 us
    reduce_scatter x2, waiting for transfers between devices, sum_mlp_out(): lax.psum_scatter(partial_term(jnp.int32(0), local_rows * lax.axis_size('t...  424 us
    reduce_scatter x4, waiting for transfers between devices, sum_attn_out(): lax.psum_scatter(partial_term(jnp.int32(0), lax.axis_size('tensor') * loc...  305 us
    all_gather x2, waiting for transfers between devices, move_norm_one(): return lax.all_gather(values, 'tensor', axis=0, tiled=True)  225 us
    reduce_scatter x2, waiting for transfers between devices, per_device(): lax.psum_scatter(jnp.einsum('tf,df->td', lax.dynamic_slice_in_dim(upward_...  224 us
    reduce_scatter x2, waiting for transfers between devices, per_device(): lax.psum_scatter(jnp.einsum('tc,dc->td', lax.dynamic_slice_in_dim(grad_pr...  222 us
    all_gather x2, waiting for transfers between devices, per_device(): lax.all_gather(branch_one.astype(jnp.bfloat16), 'tensor', axis=0, tiled=T...  173 us
    all_gather x2, waiting for transfers between devices, per_device(): lax.all_gather(branch_two.astype(jnp.bfloat16), 'tensor', axis=0, tiled=T...  163 us
  transfers between devices with their start and end apart: 25, of which 23 were waited for; matrix products, arithmetic and copies ran while one was open for 15% of the time, Pallas kernels for 0%

commit v1 on v0

v1 whole, which is shorter than its diff:
```python
import math

import jax
import jax.numpy as jnp
from jax import lax
from jax.experimental import pallas as pl
from jax.experimental.pallas import tpu as pltpu
from jax.sharding import PartitionSpec as P

HEAD_DIM = 64
SEQ = 1024
MOST_LEN = 256
PAIR = 2 * HEAD_DIM

eps_norm = 1e-06
survival = 0.9
masked_score = -1e30
score_scale = 1.0 / math.sqrt(HEAD_DIM)
groups = ("dp", "tensor")
bf16 = jnp.bfloat16
f32 = jnp.float32


def norm_forward(values, norm_gain, norm_shift):
    centre = values - jnp.mean(values, axis=-1, keepdims=True)
    spread = jnp.mean(centre * centre, axis=-1, keepdims=True)
    scaled = lax.rsqrt(spread + eps_norm)
    normalized = centre * scaled
    return (normalized * norm_gain + norm_shift, normalized, scaled)


def norm_backward(grad_out, normalized, scaled, norm_gain):
    grad_unit = grad_out * norm_gain
    inner = (
        grad_unit
        - jnp.mean(grad_unit, axis=-1, keepdims=True)
        - normalized * jnp.mean(grad_unit * normalized, axis=-1, keepdims=True)
    )
    return (inner * scaled, jnp.sum(grad_out * normalized, axis=0), jnp.sum(grad_out, axis=0))


def key_window(block):
    return max(0, (block - 1) * MOST_LEN), min(SEQ, (block + 2) * MOST_LEN)


def own_lanes(head):
    lane = lax.broadcasted_iota(jnp.int32, (1, PAIR), 1)
    return lane < HEAD_DIM if head == 0 else lane >= HEAD_DIM


def dot_rows(left, right):
    return lax.dot_general(left, right, (((1,), (1,)), ((), ())), preferred_element_type=f32)


def dot_tokens(left, right):
    return lax.dot_general(left, right, (((0,), (0,)), ((), ())), preferred_element_type=f32)


def attention_forward_kernel(q_ref, k_ref, v_ref, fq_ref, fk_ref, mixed_ref, total_ref):
    for block in range(SEQ // MOST_LEN):
        rows = slice(block * MOST_LEN, (block + 1) * MOST_LEN)
        keys = slice(*key_window(block))
        mixed = []
        totals = []
        for head in (0, 1):
            own = own_lanes(head)
            query = jnp.where(own, q_ref[rows, :] * bf16(score_scale), fq_ref[rows, :])
            key = jnp.where(own, k_ref[keys, :], fk_ref[keys, :])
            scores = dot_rows(query, key)
            top = jnp.max(scores, axis=-1, keepdims=True)
            exponent = jnp.exp(scores - top)
            total = jnp.sum(exponent, axis=-1, keepdims=True)
            part = jnp.dot(exponent.astype(bf16), v_ref[keys, :], preferred_element_type=f32)
            mixed.append(part / total)
            totals.append(top + jnp.log(total))
        own = own_lanes(0)
        mixed_ref[rows, :] = jnp.where(own, mixed[0], mixed[1]).astype(bf16)
        total_ref[rows, :] = jnp.where(own, totals[0], totals[1])


def attention_backward_kernel(
    q_ref, k_ref, v_ref, fq_ref, fk_ref, grad_ref, total_ref,
    dq_ref, dk_ref, dv_ref, sums_ref, dk_acc, dv_acc,
):
    dk_acc[...] = jnp.zeros_like(dk_acc)
    dv_acc[...] = jnp.zeros_like(dv_acc)
    query_sum = jnp.zeros((1, PAIR), f32)
    for block in range(SEQ // MOST_LEN):
        rows = slice(block * MOST_LEN, (block + 1) * MOST_LEN)
        keys = slice(*key_window(block))
        grad_query = jnp.zeros((MOST_LEN, PAIR), f32)
        for head in (0, 1):
            own = own_lanes(head)
            scaled = q_ref[rows, :] * bf16(score_scale)
            query = jnp.where(own, scaled, fq_ref[rows, :])
            key = jnp.where(own, k_ref[keys, :], fk_ref[keys, :])
            scores = dot_rows(query, key)
            lane = head * HEAD_DIM
            weights = jnp.exp(scores - total_ref[rows, lane : lane + 1])
            zero = jnp.zeros((), bf16)
            grad = jnp.where(own, grad_ref[rows, :], zero)
            product = weights * dot_rows(grad, v_ref[keys, :])
            inner = jnp.sum(product, axis=-1, keepdims=True)
            grad_scores = (product - weights * inner).astype(bf16)
            grad_query += jnp.dot(
                grad_scores, jnp.where(own, k_ref[keys, :], zero), preferred_element_type=f32
            )
            dk_acc[keys, :] += dot_tokens(grad_scores, jnp.where(own, scaled, zero))
            dv_acc[keys, :] += dot_tokens(weights.astype(bf16), grad)
        grad_query *= score_scale
        query_sum += jnp.sum(grad_query, axis=0, keepdims=True)
        dq_ref[rows, :] = grad_query.astype(bf16)
    dk_ref[...] = dk_acc[...].astype(bf16)
    dv_ref[...] = dv_acc[...].astype(bf16)
    value_sum = jnp.sum(dv_acc[...], axis=0, keepdims=True)
    row = lax.broadcasted_iota(jnp.int32, (8, PAIR), 0)
    sums_ref[0, :, :] = jnp.where(row == 0, query_sum, value_sum)


def attention_specs(pairs):
    def part(index):
        return pl.BlockSpec((SEQ, PAIR), lambda r, p: (r, index * pairs + p))

    feature = pl.BlockSpec((SEQ, PAIR), lambda r, p: (r, 0))
    own = pl.BlockSpec((SEQ, PAIR), lambda r, p: (r, p))
    return [part(0), part(1), part(2), feature, feature], own


def attention_forward(project, feature_q, feature_k):
    tokens, width = project.shape[0], project.shape[1] // 3
    pairs = width // PAIR
    ins, own = attention_specs(pairs)
    return pl.pallas_call(
        attention_forward_kernel,
        grid=(tokens // SEQ, pairs),
        in_specs=ins,
        out_specs=[own, own],
        out_shape=[
            jax.ShapeDtypeStruct((tokens, width), bf16),
            jax.ShapeDtypeStruct((tokens, width), f32),
        ],
        cost_estimate=pl.CostEstimate(
            flops=4 * tokens * 3 * MOST_LEN * 2 * width,
            bytes_accessed=tokens * width * 12,
            transcendentals=tokens * 3 * MOST_LEN * width // HEAD_DIM,
        ),
        compiler_params=pltpu.CompilerParams(vmem_limit_bytes=48 << 20),
        name="attend",
    )(project, project, project, feature_q, feature_k)


def attention_backward(project, feature_q, feature_k, grad_mixed, totals):
    tokens, width = grad_mixed.shape
    pairs = width // PAIR
    ins, own = attention_specs(pairs)
    low = jax.ShapeDtypeStruct((tokens, width), bf16)
    return pl.pallas_call(
        attention_backward_kernel,
        grid=(tokens // SEQ, pairs),
        in_specs=ins + [own, own],
        out_specs=[own, own, own, pl.BlockSpec((1, 8, PAIR), lambda r, p: (r, 0, p))],
        out_shape=[low, low, low, jax.ShapeDtypeStruct((tokens // SEQ, 8, width), f32)],
        scratch_shapes=[pltpu.VMEM((SEQ, PAIR), f32), pltpu.VMEM((SEQ, PAIR), f32)],
        cost_estimate=pl.CostEstimate(
            flops=10 * tokens * 3 * MOST_LEN * 2 * width,
            bytes_accessed=tokens * width * 18,
            transcendentals=tokens * 3 * MOST_LEN * width // HEAD_DIM,
        ),
        compiler_params=pltpu.CompilerParams(vmem_limit_bytes=48 << 20),
        name="attend_back",
    )(project, project, project, feature_q, feature_k, grad_mixed, totals)


def per_device(
    tokens,
    cotangent,
    lengths,
    drop_mask,
    ln1_gain,
    ln1_bias,
    w_qkv,
    b_qv,
    w_out,
    b_out,
    ln2_gain,
    ln2_bias,
    w_up,
    b_up,
    w_down,
    b_down,
):
    layer_count = w_qkv.shape[0]
    local_rows, width = tokens.shape
    segment_count = lengths.shape[1]
    tensor_index = lax.axis_index("tensor")
    dp_index = lax.axis_index("dp")
    n_dp = lax.axis_size("dp")
    n_tensor = lax.axis_size("tensor")
    own_rows = local_rows // SEQ
    head_cols = w_qkv.shape[3]
    hidden_cols = w_up.shape[2]
    piece = width // n_dp
    out_piece = head_cols // n_dp
    hidden_piece = hidden_cols // n_dp

    own_lengths = lax.dynamic_slice_in_dim(lengths, tensor_index * own_rows, own_rows, 0)
    own_mask = lax.dynamic_slice_in_dim(drop_mask, tensor_index * own_rows, own_rows, 2)
    segment_ends = jnp.cumsum(own_lengths, axis=-1)
    positions = jnp.arange(SEQ, dtype=jnp.int32)
    segments = jnp.sum(
        (positions[None, :, None] >= segment_ends[:, None, :]).astype(jnp.int32), axis=-1
    )
    onehot = (
        segments[:, :, None] == jnp.arange(segment_count, dtype=jnp.int32)[None, None, :]
    ).astype(f32)
    keep = (
        jnp.sum(onehot[None, None] * own_mask.astype(f32)[:, :, :, None, :], axis=-1) / survival
    ).reshape(layer_count, 2, local_rows)
    lane = jnp.arange(PAIR, dtype=jnp.int32)[None, :] % HEAD_DIM
    same = segments.reshape(local_rows, 1) == lane
    feature_q = same.astype(bf16)
    feature_k = jnp.where(same | (lane >= segment_count), 0.0, masked_score).astype(bf16)

    def gather(piece_in):
        gathered = lax.all_gather(piece_in, groups, axis=0, tiled=False)
        return gathered.reshape((n_dp, n_tensor) + piece_in.shape)

    def part_of(array, size, axis):
        return lax.dynamic_slice_in_dim(array, dp_index * size, size, axis)

    full_qkv, full_out, full_up, full_down = [], [], [], []
    for layer in range(layer_count):
        got = gather(part_of(w_qkv[layer], piece, 0).reshape(piece, 3 * head_cols))
        got = got.reshape(n_dp, n_tensor, piece, 3, head_cols).transpose(0, 2, 3, 1, 4)
        full_qkv.append(got.reshape(width, 3 * n_tensor * head_cols))
        rest = jnp.concatenate(
            [
                part_of(w_up[layer], piece, 0),
                part_of(w_down[layer], hidden_piece, 0),
                part_of(w_out[layer], out_piece, 0),
            ],
            axis=0,
        )
        got = gather(rest)
        full_up.append(
            got[:, :, :piece].transpose(0, 2, 1, 3).reshape(width, n_tensor * hidden_cols)
        )
        full_down.append(
            got[:, :, piece : piece + hidden_piece]
            .transpose(1, 0, 2, 3)
            .reshape(n_tensor * hidden_cols, width)
        )
        full_out.append(
            got[:, :, piece + hidden_piece :]
            .transpose(1, 0, 2, 3)
            .reshape(n_tensor * head_cols, width)
        )
    all_bias = lax.all_gather(
        jnp.concatenate([b_qv.reshape(-1), b_up.reshape(-1)]), "tensor", axis=0, tiled=False
    ).astype(f32)
    qv_count = layer_count * 2 * head_cols
    bias_qv = (
        all_bias[:, :qv_count]
        .reshape(n_tensor, layer_count, 2, head_cols)
        .transpose(1, 2, 0, 3)
        .reshape(layer_count, 2, width)
    )
    bias_up = (
        all_bias[:, qv_count:]
        .reshape(n_tensor, layer_count, hidden_cols)
        .transpose(1, 0, 2)
        .reshape(layer_count, n_tensor * hidden_cols)
    )

    hidden = tokens.astype(f32)
    produced = []
    kept = []
    for layer in range(layer_count):
        normed_one, unit_one, scaled_one = norm_forward(hidden, ln1_gain[layer], ln1_bias[layer])
        normed_one = normed_one.astype(bf16)
        bias = jnp.concatenate([bias_qv[layer, 0], jnp.zeros((width,), f32), bias_qv[layer, 1]])
        project = (
            jnp.dot(normed_one, full_qkv[layer], preferred_element_type=f32) + bias
        ).astype(bf16)
        mixed, totals = attention_forward(project, feature_q, feature_k)
        attn = jnp.dot(mixed, full_out[layer], preferred_element_type=f32)
        middle = hidden + keep[layer, 0][:, None] * (attn + b_out[layer].astype(f32))
        normed_two, unit_two, scaled_two = norm_forward(middle, ln2_gain[layer], ln2_bias[layer])
        normed_two = normed_two.astype(bf16)
        upward = jnp.dot(normed_two, full_up[layer], preferred_element_type=f32) + bias_up[layer]
        phi = 0.5 * (1.0 + lax.erf(upward * math.sqrt(0.5)))
        active = (upward * phi).astype(bf16)
        slope = phi + upward * (jnp.exp(-0.5 * upward * upward) * (1.0 / math.sqrt(2 * math.pi)))
        down = jnp.dot(active, full_down[layer], preferred_element_type=f32)
        hidden = middle + keep[layer, 1][:, None] * (down + b_down[layer].astype(f32))
        produced.append(hidden.astype(bf16))
        kept.append(
            (unit_one, scaled_one, normed_one, project, totals, mixed,
             unit_two, scaled_two, normed_two, active, slope)
        )
    blocks_out = jnp.stack(produced)

    def by_block(grad, columns):
        return (
            grad.astype(bf16)
            .reshape(n_dp, piece, n_tensor, columns)
            .transpose(0, 2, 1, 3)
        )

    def scatter(blocks):
        flat = blocks.reshape((n_dp * n_tensor * blocks.shape[2],) + blocks.shape[3:])
        return lax.psum_scatter(flat, groups, scatter_dimension=0, tiled=True).astype(f32)

    grad_flow = cotangent.astype(f32)
    collected = [None] * layer_count
    for layer in reversed(range(layer_count)):
        (unit_one, scaled_one, normed_one, project, totals, mixed,
         unit_two, scaled_two, normed_two, active, slope) = kept[layer]
        branch_two = keep[layer, 1][:, None] * grad_flow
        grad_bias_down = jnp.sum(branch_two, axis=0)
        branch_two = branch_two.astype(bf16)
        grad_down = by_block(dot_tokens(branch_two, active), hidden_cols)
        grad_up = dot_rows(branch_two, full_down[layer]) * slope
        grad_bias_up = jnp.sum(grad_up, axis=0)
        grad_up = grad_up.astype(bf16)
        grad_w_up = by_block(dot_tokens(normed_two, grad_up), hidden_cols)
        wide = scatter(jnp.concatenate([grad_w_up, grad_down], axis=2))
        grad_part, grad_gain_two, grad_shift_two = norm_backward(
            dot_rows(grad_up, full_up[layer]), unit_two, scaled_two, ln2_gain[layer]
        )
        grad_middle = grad_flow + grad_part
        branch_one = keep[layer, 0][:, None] * grad_middle
        grad_bias_out = jnp.sum(branch_one, axis=0)
        branch_one = branch_one.astype(bf16)
        grad_out = by_block(dot_tokens(branch_one, mixed), head_cols)
        grad_mixed = dot_rows(branch_one, full_out[layer]).astype(bf16)
        *grads, sums = attention_backward(project, feature_q, feature_k, grad_mixed, totals)
        grad_bias_qv = jnp.sum(sums, axis=0)[:2]
        weights = full_qkv[layer].reshape(width, 3, width)
        grad_one = sum(dot_rows(grads[part], weights[:, part]) for part in range(3))
        narrow = [by_block(dot_tokens(normed_one, grad), head_cols) for grad in grads]
        narrow = scatter(jnp.concatenate(narrow + [grad_out], axis=3))
        grad_part, grad_gain_one, grad_shift_one = norm_backward(
            grad_one, unit_one, scaled_one, ln1_gain[layer]
        )
        grad_flow = grad_middle + grad_part
        collected[layer] = (
            jnp.concatenate(
                [grad_gain_one, grad_shift_one, grad_bias_qv.reshape(-1), grad_bias_out,
                 grad_gain_two, grad_shift_two, grad_bias_down, grad_bias_up]
            ),
            narrow[:, : 3 * head_cols].reshape(piece, 3, head_cols),
            narrow[:, 3 * head_cols :].T,
            wide[:piece],
            wide[piece:].T,
        )
    small, grad_qkv, grad_out, grad_up, grad_down = [
        jnp.stack([entry[position] for entry in collected]) for position in range(5)
    ]
    small = lax.psum(small, groups)
    gain_one, shift_one, query_bias, value_bias, bias_out, gain_two, shift_two, bias_down = [
        small[:, position * width : (position + 1) * width] for position in range(8)
    ]
    return (
        blocks_out,
        grad_flow,
        gain_one,
        shift_one,
        grad_qkv,
        jnp.stack([query_bias, value_bias], axis=1),
        grad_out,
        bias_out,
        gain_two,
        shift_two,
        grad_up,
        small[:, 8 * width :],
        grad_down,
        bias_down,
    )


def solution(mesh):
    in_specs = (
        P(("dp", "tensor"), None),
        P(("dp", "tensor"), None),
        P("dp", None),
        P(None, None, "dp", None),
        P(),
        P(),
        P(None, None, None, "tensor"),
        P(None, None, "tensor"),
        P(None, "tensor", None),
        P(),
        P(),
        P(),
        P(None, None, "tensor"),
        P(None, "tensor"),
        P(None, "tensor", None),
        P(),
    )
    out_specs = (
        P(None, ("dp", "tensor"), None),
        P(("dp", "tensor"), None),
        P(),
        P(),
        P(None, "dp", None, "tensor"),
        P(),
        P(None, "tensor", "dp"),
        P(),
        P(),
        P(),
        P(None, "dp", "tensor"),
        P(),
        P(None, "tensor", "dp"),
        P(),
    )
    return jax.shard_map(
        per_device, mesh=mesh, in_specs=in_specs, out_specs=out_specs, check_vma=False
    )
```

time: 3610 us -> 1260 us (0.35)
  waiting for transfers between devices: 2380 us -> 575 us
  matrix products: 767 us -> 181 us
  other arithmetic: 209 us -> 80.7 us
  Pallas kernels: 0 us -> 114 us
  local copies, waits for them, and re-layouts: 218 us -> 268 us
    all_gather x10 -> x4, waiting for transfers between devices: 1000 us -> 172 us  [gather(): gathered = lax.all_gather(piece_in, groups, axis=0, tiled=False)]
    reduce_scatter x11 -> x4, waiting for transfers between devices: 1230 us -> 403 us  [scatter(): lax.psum_scatter(flat, groups, scatter_dimension=0, tiled=True).astype(f32)]
    dot_general x154 -> x32, matrix products: 670 us -> 181 us  [the longest x12 64.4 us: dot_rows(): lax.dot_general(left, right, (((1,), (1,)), ((), ())), preferred_element_...]
    psum x1, waiting for transfers between devices: 134 us -> 0.01 us  [per_device(): small = lax.psum(small, groups)]
    pallas_call x0 -> x4, Pallas kernels: none -> 114 us  [the longest x2 73 us: attention_backward(): pl.pallas_call(attention_backward_kernel, grid=(tokens // SEQ, pairs), in...]
    reshape x2 -> x29, local copies, waits for them, and re-layouts: 2.38 us -> 107 us  [the longest x20 89.6 us: by_block(): return grad.astype(bf16).reshape(n_dp, piece, n_tensor, columns).transpos...]
    sub x16 -> x0, matrix products: 97.2 us -> none  [one_row(): exponent = jnp.exp(scores - row_top)]
    convert_element_type x32 -> x8, other arithmetic: 73.5 us -> 3.65 us  [the longest x4 2.04 us: scatter(): lax.psum_scatter(flat, groups, scatter_dimension=0, tiled=True).astype(f32)]
  transfers between devices with their start and end apart: 25 -> 9, of which waited for: 23 -> 8; matrix products, arithmetic and copies ran while one was open for 15% -> 25% of each run, Pallas kernels for 0% -> 2%
where the time goes in v1:
time: 1260 us; the launch traced here: 1250 us
  waiting for transfers between devices  575 us (46%)
  local copies, waits for them, and re-layouts  268 us (21%)
  matrix products  181 us (14%)
  Pallas kernels  114 us (9%)
  other arithmetic  80.7 us (6%)
  between operations  15.9 us (1%)
  blocking collectives  13.4 us (1%)
    reduce_scatter x4, waiting for transfers between devices, scatter(): lax.psum_scatter(flat, groups, scatter_dimension=0, tiled=True).astype(f32)  403 us
    all_gather x4, waiting for transfers between devices, gather(): gathered = lax.all_gather(piece_in, groups, axis=0, tiled=False)  172 us
    reshape x20, local copies, waits for them, and re-layouts, by_block(): return grad.astype(bf16).reshape(n_dp, piece, n_tensor, columns).transpos...  89.6 us
    pallas_call x2, Pallas kernels, attention_backward(): pl.pallas_call(attention_backward_kernel, grid=(tokens // SEQ, pairs), in...  73 us
    dot_general x12, matrix products, dot_rows(): lax.dot_general(left, right, (((1,), (1,)), ((), ())), preferred_element_...  64.4 us
    dot_general x12, matrix products, dot_tokens(): lax.dot_general(left, right, (((0,), (0,)), ((), ())), preferred_element_...  63.8 us
    unnamed x241, local copies, waits for them, and re-layouts  41.1 us
    pallas_call x2, Pallas kernels, attention_forward(): pl.pallas_call(attention_forward_kernel, grid=(tokens // SEQ, pairs), in_...  40.8 us
  transfers between devices with their start and end apart: 9, of which 8 were waited for; matrix products, arithmetic and copies ran while one was open for 25% of the time, Pallas kernels for 2%

profile of v1, /device:TPU:8, one launch (start us, length us, event | category | flops | bytes accessed | tf_op | source)
XLA Modules:
  0.0 1248.4 jit_solution(6675335244740168568)
XLA Ops:
  18.1 13.4 %all-gather.3 = bf16[4,1,2304]{2,1,0:T(2,128)(2,1)S(1)} all-gather(bf16[1,1,2304]{2,1,0:T(2,128)(2,1)S(1)} %reshape.389), channel_id=2, replica_groups=mesh['dp'=8,'tensor'=4] {'tensor'}, dimensions={0}, use_global_device_ids=true | all-gather | bytes 23040 | tf_op jit(solution)/shard_map/all_gather | solution.py:258
  39.2 34.6 %all-gather.9.cloned.1.call-done = bf16[32,96,576]{2,1,0:T(8,128)(2,1)} async-done(((bf16[1,96,576]{2,1,0:T(8,128)(2,1)}), bf16[32,96,576]{2,1,0:T(8,128)(2,1)}) %all-gather.9.cloned.1.call-update) | async-done | bytes 3538960 | tf_op jit(solution)/shard_map/all_gather | solution.py:225
  105.6 31.5 %all-gather.11.cloned.1.call-done = bf16[32,96,576]{2,1,0:T(8,128)(2,1)} async-done(((bf16[1,96,576]{2,1,0:T(8,128)(2,1)}), bf16[32,96,576]{2,1,0:T(8,128)(2,1)}) %all-gather.11.cloned.1.call-update) | async-done | bytes 3538960 | tf_op jit(solution)/shard_map/all_gather | solution.py:225
  160.9 8.4 reshape.356
  177.4 20.4 %attend.2 = (bf16[1024,768]{1,0:T(8,128)(2,1)S(1)}, f32[1024,768]{1,0:T(8,128)S(1)}) custom-call(bf16[1024,2304]{1,0:T(8,128)(2,1)} %add_convert_fusion.1.q_ref.k_ref.v_ref, bf16[1024,2304]{1,0:T(8,128)(2,1)} %add_convert_fusion.1.q_ref.k_ref.v_ref, bf16[1024,2304]{1,0:T(8,128)(2,1)} %add_convert_fusion.1.q_ref.k_ref.v_ref, ...), custom_call_target="tpu_custom_call" | custom-call | flops 4831838208 | bytes 9437184 | tf_op jit(solution)/shard_map/attend/pallas_call | solution.py:133
  199.5 26.8 %all-gather.15.cloned.1.call-done = bf16[6912,768]{1,0:T(8,128)(2,1)} async-done(((bf16[216,768]{1,0:T(8,128)(2,1)}), bf16[6912,768]{1,0:T(8,128)(2,1)}) %all-gather.15.cloned.1.call-update) | async-done | bytes 10616848 | tf_op jit(solution)/shard_map/all_gather | solution.py:225
  235.9 79.2 %all-gather.13.cloned.1.call-done = bf16[6912,768]{1,0:T(8,128)(2,1)} async-done(((bf16[216,768]{1,0:T(8,128)(2,1)}), bf16[6912,768]{1,0:T(8,128)(2,1)}) %all-gather.13.cloned.1.call-update) | async-done | bytes 10616848 | tf_op jit(solution)/shard_map/all_gather | solution.py:225
  316.6 8.4 slice_bitcast_fusion.2
  348.4 10.0 multiply_convert_fusion.1
  373.6 20.4 %attend.3 = (bf16[1024,768]{1,0:T(8,128)(2,1)S(1)}, f32[1024,768]{1,0:T(8,128)S(1)}) custom-call(bf16[1024,2304]{1,0:T(8,128)(2,1)} %add_convert_fusion.q_ref.k_ref.v_ref, bf16[1024,2304]{1,0:T(8,128)(2,1)} %add_convert_fusion.q_ref.k_ref.v_ref, bf16[1024,2304]{1,0:T(8,128)(2,1)} %add_convert_fusion.q_ref.k_ref.v_ref, ...), custom_call_target="tpu_custom_call" | custom-call | flops 4831838208 | bytes 9437184 | tf_op jit(solution)/shard_map/attend/pallas_call | solution.py:133
  398.6 10.9 multiply_convert_fusion
  409.6 11.4 fusion.61
  444.6 36.5 %attend_back.2 = (bf16[1024,768]{1,0:T(8,128)(2,1)S(1)}, bf16[1024,768]{1,0:T(8,128)(2,1)S(1)}, bf16[1024,768]{1,0:T(8,128)(2,1)S(1)}, f32[1,8,768]{2,1,0:T(8,128)S(1)}) custom-call(bf16[1024,2304]{1,0:T(8,128)(2,1)} %add_convert_fusion.q_ref.k_ref.v_ref, bf16[1024,2304]{1,0:T(8,128)(2,1)} %add_convert_fusion.q_ref.k_ref.v_ref, ...), custom_call_target="tpu_custom_call" | custom-call | flops 12079595520 | bytes 14155776 | tf_op jit(solution)/shard_map/attend_back/pallas_call | solution.py:157
  527.1 13.4 %fusion.63 = (f32[3072]{0:T(1024)S(1)}, bf16[1024,3072]{1,0:T(8,128)(2,1)S(1)}) fusion(f32[1024,3072]{1,0:T(8,128)} %get-tuple-element.195, f32[3072]{0:T(1024)S(1)} %bitcast.288, bf16[3072,768]{1,0:T(8,128)(2,1)} %bitcast.243, f32[1024,768]{0,1:T(8,128)S(1)} %get-tuple-element.153, f32[1024]{0:T(1024)S(1)} %bitcast.285), kind=kOutput, calls=%fused_computation.229 | convolution fusion | flops 4871156736 | bytes 26767360 | tf_op jit(solution)/shard_map/dot_general | solution.py:52
  561.7 36.5 %attend_back.3 = (bf16[1024,768]{1,0:T(8,128)(2,1)S(1)}, bf16[1024,768]{1,0:T(8,128)(2,1)S(1)}, bf16[1024,768]{1,0:T(8,128)(2,1)S(1)}, f32[1,8,768]{2,1,0:T(8,128)S(1)}) custom-call(bf16[1024,2304]{1,0:T(8,128)(2,1)} %add_convert_fusion.1.q_ref.k_ref.v_ref, bf16[1024,2304]{1,0:T(8,128)(2,1)} %add_convert_fusion.1.q_ref.k_ref.v_ref, ...), custom_call_target="tpu_custom_call" | custom-call | flops 12079595520 | bytes 14155776 | tf_op jit(solution)/shard_map/attend_back/pallas_call | solution.py:157
  667.6 9.5 convolution_convert_fusion
  677.1 9.9 reshape.377
  687.1 9.8 convolution_convert_fusion.1
  696.8 9.7 reshape.376
  706.6 16.9 %pad_maximum_fusion.1 = bf16[8,4,192,768]{3,1,2,0:T(4,128)(2,1)} fusion(bf16[8,4,96,768]{3,1,2,0:T(4,128)(2,1)} %bitcast.222, bf16[8,4,96,768]{3,1,2,0:T(4,128)(2,1)} %bitcast.225), kind=kLoop, calls=%fused_computation.17 | loop fusion | flops 4718592 | bytes 18874368 | tf_op jit(solution)/shard_map/concatenate | solution.py:327
  723.5 9.2 copy.290
  734.6 9.7 convolution_convert_fusion.2
  744.2 10.0 reshape.374
  754.2 9.9 convolution_convert_fusion.3
  764.1 9.8 reshape.373
  773.9 16.9 %pad_maximum_fusion = bf16[8,4,192,768]{3,1,2,0:T(4,128)(2,1)} fusion(bf16[8,4,96,768]{3,1,2,0:T(4,128)(2,1)} %bitcast.221, bf16[8,4,96,768]{3,1,2,0:T(4,128)(2,1)} %bitcast.226), kind=kLoop, calls=%fused_computation.16 | loop fusion | flops 4718592 | bytes 18874368 | tf_op jit(solution)/shard_map/concatenate | solution.py:327
  790.9 9.2 copy.289
  802.0 9.1 fusion.32
  830.2 13.9 %reduce-scatter.7.cloned.1.call-done = bf16[96,768]{1,0:T(8,128)(2,1)} async-done(((bf16[3072,768]{1,0:T(8,128)(2,1)}), bf16[96,768]{1,0:T(8,128)(2,1)}) %reduce-scatter.7.cloned.1.call-update) | async-done | bytes 147472 | tf_op jit(solution)/shard_map/reduce_scatter | solution.py:312
  845.3 110.8 %reduce-scatter.5.cloned.1.call-done = bf16[96,768]{1,0:T(8,128)(2,1)} async-done(((bf16[3072,768]{1,0:T(8,128)(2,1)}), bf16[96,768]{1,0:T(8,128)(2,1)}) %reduce-scatter.5.cloned.1.call-update) | async-done | bytes 147472 | tf_op jit(solution)/shard_map/reduce_scatter | solution.py:312
  959.5 137.9 %reduce-scatter.11.cloned.1.call-done = bf16[192,768]{1,0:T(8,128)(2,1)} async-done(((bf16[6144,768]{1,0:T(8,128)(2,1)}), bf16[192,768]{1,0:T(8,128)(2,1)}) %reduce-scatter.11.cloned.1.call-update) | async-done | bytes 294928 | tf_op jit(solution)/shard_map/reduce_scatter | solution.py:312
  1098.4 140.3 %reduce-scatter.9.cloned.1.call-done = bf16[192,768]{1,0:T(8,128)(2,1)} async-done(((bf16[6144,768]{1,0:T(8,128)(2,1)}), bf16[192,768]{1,0:T(8,128)(2,1)}) %reduce-scatter.9.cloned.1.call-update) | async-done | bytes 294928 | tf_op jit(solution)/shard_map/reduce_scatter | solution.py:312
  (428 shorter events, 328.3 us)
Async XLA Ops:
  7.2 24.4 %copy-start = (s32[4,6]{1,0:T(4,128)S(1)}, s32[4,6]{1,0:T(4,128)}, u32[]{:S(2)}) copy-start(s32[4,6]{1,0:T(4,128)} %param.18) | copy-start | bytes 292
  7.2 66.7 %all-gather.9.cloned.1.call-start = ((), (), s32[]{:S(2)}) async-start(), calls=%async_computation.4 | async-start | bytes 4055040 | tf_op jit(solution)/shard_map/all_gather | solution.py:225
  11.8 125.2 %all-gather.11.cloned.1.call-start = ((), (), s32[]{:S(2)}) async-start(), calls=%async_computation.5 | async-start | bytes 4055040 | tf_op jit(solution)/shard_map/all_gather | solution.py:225
  12.7 213.6 %all-gather.15.cloned.1.call-start = ((), (), s32[]{:S(2)}) async-start(), calls=%async_computation.12 | async-start | bytes 10948608 | tf_op jit(solution)/shard_map/all_gather | solution.py:225
  15.2 17.6 %copy-start.44 = (bf16[1024,768]{1,0:T(8,128)(2,1)S(1)}, bf16[1024,768]{1,0:T(8,128)(2,1)}, u32[]{:S(2)}) copy-start(bf16[1024,768]{1,0:T(8,128)(2,1)} %param.16) | copy-start | bytes 4718596
  16.2 298.9 %all-gather.13.cloned.1.call-start = ((), (), s32[]{:S(2)}) async-start(), calls=%async_computation.11 | async-start | bytes 10948608 | tf_op jit(solution)/shard_map/all_gather | solution.py:225
  18.0 808.9 %all-reduce.2.cloned.1.call-start = ((), (), s32[]{:S(2)}) async-start(), calls=%async_computation.6 | async-start | bytes 147456 | tf_op jit(solution)/shard_map/psum | solution.py:360
  33.7 135.6 %copy-start.22 = (bf16[1024,768]{0,1:T(8,128)(2,1)}, bf16[1024,768]{0,1:T(8,128)(2,1)S(1)}, u32[]{:S(2)}) copy-start(bf16[1024,768]{0,1:T(8,128)(2,1)S(1)} %copy.243) | copy-start | bytes 4718596
  37.6 131.6 %copy-start.66 = (f32[768]{0:T(1024)}, f32[768]{0:T(1024)S(1)}, u32[]{:S(2)}) copy-start(f32[768]{0:T(1024)S(1)} %get-tuple-element.218) | copy-start | bytes 9220
  37.7 131.6 %copy-start.83 = (f32[768]{0:T(1024)}, f32[768]{0:T(1024)S(1)}, u32[]{:S(2)}) copy-start(f32[768]{0:T(1024)S(1)} %get-tuple-element.147) | copy-start | bytes 9220
  37.7 310.7 %copy-start.58 = (f32[768]{0:T(1024)}, f32[768]{0:T(1024)S(1)}, u32[]{:S(2)}) copy-start(f32[768]{0:T(1024)S(1)} %get-tuple-element.220) | copy-start | bytes 9220
  37.7 310.7 %copy-start.79 = (f32[768]{0:T(1024)}, f32[768]{0:T(1024)S(1)}, u32[]{:S(2)}) copy-start(f32[768]{0:T(1024)S(1)} %get-tuple-element.143) | copy-start | bytes 9220
  37.7 358.5 %copy-start.81 = (f32[768]{0:T(1024)}, f32[768]{0:T(1024)S(1)}, u32[]{:S(2)}) copy-start(f32[768]{0:T(1024)S(1)} %get-tuple-element.142) | copy-start | bytes 9220
  38.3 131.0 %copy-start.60 = (f32[1024]{0:T(1024)}, f32[1024]{0:T(1024)S(1)}, u32[]{:S(2)}) copy-start(f32[1024]{0:T(1024)S(1)} %broadcast_multiply_fusion.12) | copy-start | bytes 12292
  38.7 130.6 %copy-start.68 = (f32[1024]{0:T(1024)}, f32[1024]{0:T(1024)S(1)}, u32[]{:S(2)}) copy-start(f32[1024]{0:T(1024)S(1)} %add_rsqrt_fusion.3) | copy-start | bytes 12292
  38.8 307.2 %copy-start.70 = (f32[1,1,1024]{2,1,0:T(1,128)}, f32[1,1,1024]{2,1,0:T(1,128)S(1)}, u32[]{:S(2)}) copy-start(f32[1,1,1024]{2,1,0:T(1,128)S(1)} %get-tuple-element.189) | copy-start | bytes 12292
  199.5 146.5 %copy-start.4 = (bf16[1024,768]{1,0:T(8,128)(2,1)}, bf16[1024,768]{1,0:T(8,128)(2,1)S(1)}, u32[]{:S(2)}) copy-start(bf16[1024,768]{1,0:T(8,128)(2,1)S(1)} %get-tuple-element.26) | copy-start | bytes 4718596
  332.0 14.0 %copy-start.48 = (bf16[4,8,24,768]{3,2,1,0:T(8,128)(2,1)}, bf16[4,8,24,768]{3,2,1,0:T(8,128)(2,1)S(1)}, u32[]{:S(2)}) copy-start(bf16[4,8,24,768]{3,2,1,0:T(8,128)(2,1)S(1)} %copy.249) | copy-start | bytes 3538948
  363.9 30.1 %copy-start.11 = (f32[1024,768]{0,1:T(8,128)}, f32[1024,768]{0,1:T(8,128)S(1)}, u32[]{:S(2)}) copy-start(f32[1024,768]{0,1:T(8,128)S(1)} %get-tuple-element.197) | copy-start | bytes 9437188
  373.6 20.4 %copy-start.50 = (bf16[4,8,24,768]{3,2,1,0:T(8,128)(2,1)S(1)}, bf16[4,8,24,768]{3,2,1,0:T(8,128)(2,1)}, u32[]{:S(2)}) copy-start(bf16[4,8,24,768]{3,2,1,0:T(8,128)(2,1)} %copy.255) | copy-start | bytes 3538948
  395.8 13.7 %copy-start.16 = (f32[1024,768]{0,1:T(8,128)}, f32[1024,768]{0,1:T(8,128)S(1)}, u32[]{:S(2)}) copy-start(f32[1024,768]{0,1:T(8,128)S(1)} %get-tuple-element.199) | copy-start | bytes 9437188
  395.8 13.7 %slice-start.8 = ((s8[4718592]{0:T(1024)(128)(4,1)}), s8[4194304]{0:T(1024)(128)(4,1)S(1)}, s32[]{:S(2)}) async-start(s8[4718592]{0:T(1024)(128)(4,1)} %bitcast.240), calls=%async_computation.21 | async-start | bytes 8388608
  444.6 36.6 %copy-start.46 = (bf16[1024,768]{0,1:T(8,128)(2,1)S(1)}, bf16[1024,768]{0,1:T(8,128)(2,1)}, u32[]{:S(2)}) copy-start(bf16[1024,768]{0,1:T(8,128)(2,1)} %copy-done.45) | copy-start | bytes 4718596
  524.4 16.2 %slice-start.14 = ((s8[4718592]{0:T(1024)(128)(4,1)}), s8[524288]{0:T(1024)(128)(4,1)S(1)}, s32[]{:S(2)}) async-start(s8[4718592]{0:T(1024)(128)(4,1)} %bitcast.250), calls=%async_computation.27 | async-start | bytes 1048576
  527.1 13.4 %copy-start.28 = (f32[1024,768]{0,1:T(8,128)}, f32[1024,768]{0,1:T(8,128)S(1)}, u32[]{:S(2)}) copy-start(f32[1024,768]{0,1:T(8,128)S(1)} %get-tuple-element.153) | copy-start | bytes 9437188
  527.1 13.4 %slice-start.15 = ((s8[4718592]{0:T(1024)(128)(4,1)}), s8[4194304]{0:T(1024)(128)(4,1)S(1)}, s32[]{:S(2)}) async-start(s8[4718592]{0:T(1024)(128)(4,1)} %bitcast.250), calls=%async_computation.28 | async-start | bytes 8388608
  610.3 233.8 %reduce-scatter.7.cloned.1.call-start = ((), (), s32[]{:S(2)}) async-start(), calls=%async_computation.8 | async-start | bytes 4866048 | tf_op jit(solution)/shard_map/reduce_scatter | solution.py:312
  616.9 339.1 %reduce-scatter.5.cloned.1.call-start = ((), (), s32[]{:S(2)}) async-start(), calls=%async_computation.7 | async-start | bytes 4866048 | tf_op jit(solution)/shard_map/reduce_scatter | solution.py:312
  666.3 431.1 %reduce-scatter.11.cloned.1.call-start = ((), (), s32[]{:S(2)}) async-start(), calls=%async_computation.10 | async-start | bytes 9732096 | tf_op jit(solution)/shard_map/reduce_scatter | solution.py:312
  732.7 506.0 %reduce-scatter.9.cloned.1.call-start = ((), (), s32[]{:S(2)}) async-start(), calls=%async_computation.9 | async-start | bytes 9732096 | tf_op jit(solution)/shard_map/reduce_scatter | solution.py:312
  844.1 114.2 %copy-start.54 = (bf16[96,768]{1,0:T(8,128)(2,1)S(1)}, bf16[96,768]{1,0:T(8,128)(2,1)}, u32[]{:S(2)}) copy-start(bf16[96,768]{1,0:T(8,128)(2,1)} %reduce-scatter.7.cloned.1.call-done) | copy-start | bytes 442372
  958.6 282.8 %copy-start.1 = (s32[4,6]{1,0:T(4,128)S(1)}, s32[4,6]{1,0:T(4,128)}, u32[]{:S(2)}) copy-start(s32[4,6]{1,0:T(4,128)} %param.18) | copy-start | bytes 292
  (85 other events, 403.8 us)
Sparse Core Ops, SparseCore 0:
  11.9 61.9 all-gather.8
  77.3 59.7 all-gather.10
  140.4 85.8 all-gather.14
  229.5 85.4 all-gather.12
  610.4 122.0 all-reduce.1
  737.9 106.1 reduce-scatter.6
  849.6 106.4 reduce-scatter.4
  962.0 135.3 reduce-scatter.10
  1103.2 135.3 reduce-scatter.8

commit v2 on v1

--- a/solution.py
+++ b/solution.py
@@ -171,6 +171,113 @@
     )(project, project, project, feature_q, feature_k, grad_mixed, totals)
 
 
+def wide_kernel(norm_ref, up_ref, branch_ref, active_ref, *rest):
+    out_ref, turned, result = rest[-3:]
+    piece = out_ref.shape[3]
+    step = pl.program_id(0)
+    for position, (left_ref, right_ref) in enumerate(
+        ((norm_ref, up_ref), (branch_ref, active_ref))
+    ):
+
+        @pl.when(step == position)
+        def _():
+            @pl.when(pl.program_id(1) == 0)
+            def _():
+                turned[...] = left_ref[...].T
+
+            result[...] = jnp.dot(turned[...], right_ref[...], preferred_element_type=f32)
+
+    for block in range(out_ref.shape[0]):
+        out_ref[block, 0, 0] = result[block * piece : (block + 1) * piece, :].astype(bf16)
+
+
+def narrow_kernel(norm_ref, dq_ref, dk_ref, dv_ref, branch_ref, mixed_ref, *rest):
+    out_ref, turned, result = rest[-3:]
+    blocks, shards, _, piece, columns = out_ref.shape
+    columns //= 4
+    for position, right_ref in enumerate((dq_ref, dk_ref, dv_ref, mixed_ref)):
+        if position == 0:
+            turned[...] = norm_ref[...].T
+        if position == 3:
+            turned[...] = branch_ref[...].T
+        result[...] = jnp.dot(turned[...], right_ref[...], preferred_element_type=f32)
+        for block in range(blocks):
+            for shard in range(shards):
+                out_ref[block, shard, 0, :, position * columns : (position + 1) * columns] = (
+                    result[
+                        block * piece : (block + 1) * piece,
+                        shard * columns : (shard + 1) * columns,
+                    ].astype(bf16)
+                )
+
+
+def blocked_gradients(kernel, ins, in_specs, grid, out_spec, shape, store, depth, products, name):
+    tokens, width = depth, shape[-1]
+    alias = {}
+    if store is not None:
+        alias = {len(ins): 0}
+        ins = ins + [store]
+        in_specs = in_specs + [pl.BlockSpec(memory_space=pl.ANY)]
+    return pl.pallas_call(
+        kernel,
+        grid=grid,
+        in_specs=in_specs,
+        out_specs=out_spec,
+        out_shape=jax.ShapeDtypeStruct(shape, bf16),
+        scratch_shapes=[pltpu.VMEM((width, tokens), bf16), pltpu.VMEM((width, width), f32)],
+        input_output_aliases=alias,
+        cost_estimate=pl.CostEstimate(
+            flops=2 * products * tokens * width * width,
+            bytes_accessed=products * 2 * (tokens * width + width * width),
+            transcendentals=0,
+        ),
+        compiler_params=pltpu.CompilerParams(vmem_limit_bytes=56 << 20),
+        name=name,
+    )(*ins)
+
+
+def wide_gradients(normed, grad_up, branch, active, shape, store, slot):
+    tokens, width = normed.shape
+    n_dp, n_tensor, _, piece, _ = shape
+    whole = pl.BlockSpec((tokens, width), lambda s, t: (0, 0))
+    last = n_tensor - 1
+    return blocked_gradients(
+        wide_kernel,
+        [normed, grad_up, branch, active],
+        [
+            whole,
+            pl.BlockSpec((tokens, width), lambda s, t: (0, jnp.where(s == 0, t, last))),
+            whole,
+            pl.BlockSpec((tokens, width), lambda s, t: (0, jnp.where(s == 1, t, 0))),
+        ],
+        (2, n_tensor),
+        pl.BlockSpec((n_dp, 1, 1, piece, width), lambda s, t: (0, t, slot + s, 0, 0)),
+        shape,
+        store,
+        tokens,
+        2 * n_tensor,
+        "wide_grads",
+    )
+
+
+def narrow_gradients(normed, grads, branch, mixed, shape, store, slot):
+    tokens, width = normed.shape
+    n_dp, n_tensor, _, piece, _ = shape
+    whole = pl.BlockSpec((tokens, width), lambda s: (0, 0))
+    return blocked_gradients(
+        narrow_kernel,
+        [normed, *grads, branch, mixed],
+        [whole] * 6,
+        (1,),
+        pl.BlockSpec((n_dp, n_tensor, 1, piece, width), lambda s: (0, 0, slot, 0, 0)),
+        shape,
+        store,
+        tokens,
+        4,
+        "narrow_grads",
+    )
+
+
 def per_device(
     tokens,
     cotangent,
@@ -221,43 +328,52 @@
     feature_q = same.astype(bf16)
     feature_k = jnp.where(same | (lane >= segment_count), 0.0, masked_score).astype(bf16)
 
-    def gather(piece_in):
-        gathered = lax.all_gather(piece_in, groups, axis=0, tiled=False)
-        return gathered.reshape((n_dp, n_tensor) + piece_in.shape)
+    def gather(pieces):
+        rows = jnp.concatenate(pieces, axis=0)
+        gathered = lax.all_gather(rows, groups, axis=0, tiled=False)
+        return gathered.reshape((n_dp, n_tensor) + rows.shape)
 
     def part_of(array, size, axis):
         return lax.dynamic_slice_in_dim(array, dp_index * size, size, axis)
 
-    full_qkv, full_out, full_up, full_down = [], [], [], []
+    def qkv_piece(layer):
+        turned = w_qkv[layer].transpose(1, 2, 0)
+        return part_of(turned, out_piece, 1).reshape(3 * out_piece, width)
+
+    def pieces_of(layer):
+        return [
+            part_of(w_up[layer], hidden_piece, 1).T,
+            part_of(w_down[layer], hidden_piece, 0),
+            part_of(w_out[layer], out_piece, 0),
+            qkv_piece(layer),
+        ]
+
+    def rows_of(got, first, count, parts=1):
+        rows = got[:, :, first : first + parts * count]
+        rows = rows.reshape(n_dp, n_tensor, parts, count, width).transpose(2, 1, 0, 3, 4)
+        return lax.optimization_barrier(rows.reshape(parts * n_dp * n_tensor * count, width))
+
+    def weights_of(got):
+        up = rows_of(got, 0, hidden_piece)
+        down = rows_of(got, hidden_piece, hidden_piece)
+        out = rows_of(got, 2 * hidden_piece, out_piece)
+        return rows_of(got, 2 * hidden_piece + out_piece, out_piece, 3), up, down, out
+
+    weight_rows = 2 * hidden_piece + 4 * out_piece
+    bias_rows = jnp.concatenate([b_qv.reshape(-1), b_up.reshape(-1)])
+    bias_rows = jnp.pad(bias_rows, (0, 8 * width - bias_rows.shape[0])).reshape(8, width)
+    full = []
     for layer in range(layer_count):
-        got = gather(part_of(w_qkv[layer], piece, 0).reshape(piece, 3 * head_cols))
-        got = got.reshape(n_dp, n_tensor, piece, 3, head_cols).transpose(0, 2, 3, 1, 4)
-        full_qkv.append(got.reshape(width, 3 * n_tensor * head_cols))
-        rest = jnp.concatenate(
-            [
-                part_of(w_up[layer], piece, 0),
-                part_of(w_down[layer], hidden_piece, 0),
-                part_of(w_out[layer], out_piece, 0),
-            ],
-            axis=0,
-        )
-        got = gather(rest)
-        full_up.append(
-            got[:, :, :piece].transpose(0, 2, 1, 3).reshape(width, n_tensor * hidden_cols)
-        )
-        full_down.append(
-            got[:, :, piece : piece + hidden_piece]
-            .transpose(1, 0, 2, 3)
-            .reshape(n_tensor * hidden_cols, width)
-        )
-        full_out.append(
-            got[:, :, piece + hidden_piece :]
-            .transpose(1, 0, 2, 3)
-            .reshape(n_tensor * head_cols, width)
-        )
-    all_bias = lax.all_gather(
-        jnp.concatenate([b_qv.reshape(-1), b_up.reshape(-1)]), "tensor", axis=0, tiled=False
-    ).astype(f32)
+        pieces = pieces_of(layer)
+        if layer == 0:
+            got = gather(pieces + [bias_rows])
+            all_bias = got[0, :, weight_rows:].reshape(n_tensor, 8 * width).astype(f32)
+        else:
+            pieces, got = lax.optimization_barrier((pieces, got))
+            full.append(weights_of(got))
+            got = gather(pieces)
+    full.append(weights_of(got))
+
     qv_count = layer_count * 2 * head_cols
     bias_qv = (
         all_bias[:, :qv_count]
@@ -266,7 +382,7 @@
         .reshape(layer_count, 2, width)
     )
     bias_up = (
-        all_bias[:, qv_count:]
+        all_bias[:, qv_count : qv_count + layer_count * hidden_cols]
         .reshape(n_tensor, layer_count, hidden_cols)
         .transpose(1, 0, 2)
         .reshape(layer_count, n_tensor * hidden_cols)
@@ -279,19 +395,18 @@
         normed_one, unit_one, scaled_one = norm_forward(hidden, ln1_gain[layer], ln1_bias[layer])
         normed_one = normed_one.astype(bf16)
         bias = jnp.concatenate([bias_qv[layer, 0], jnp.zeros((width,), f32), bias_qv[layer, 1]])
-        project = (
-            jnp.dot(normed_one, full_qkv[layer], preferred_element_type=f32) + bias
-        ).astype(bf16)
+        full_qkv, full_up, full_down, full_out = full[layer]
+        project = (dot_rows(normed_one, full_qkv) + bias).astype(bf16)
         mixed, totals = attention_forward(project, feature_q, feature_k)
-        attn = jnp.dot(mixed, full_out[layer], preferred_element_type=f32)
+        attn = jnp.dot(mixed, full_out, preferred_element_type=f32)
         middle = hidden + keep[layer, 0][:, None] * (attn + b_out[layer].astype(f32))
         normed_two, unit_two, scaled_two = norm_forward(middle, ln2_gain[layer], ln2_bias[layer])
         normed_two = normed_two.astype(bf16)
-        upward = jnp.dot(normed_two, full_up[layer], preferred_element_type=f32) + bias_up[layer]
+        upward = dot_rows(normed_two, full_up) + bias_up[layer]
         phi = 0.5 * (1.0 + lax.erf(upward * math.sqrt(0.5)))
         active = (upward * phi).astype(bf16)
         slope = phi + upward * (jnp.exp(-0.5 * upward * upward) * (1.0 / math.sqrt(2 * math.pi)))
-        down = jnp.dot(active, full_down[layer], preferred_element_type=f32)
+        down = jnp.dot(active, full_down, preferred_element_type=f32)
         hidden = middle + keep[layer, 1][:, None] * (down + b_down[layer].astype(f32))
         produced.append(hidden.astype(bf16))
         kept.append(
@@ -300,64 +415,87 @@
         )
     blocks_out = jnp.stack(produced)
 
-    def by_block(grad, columns):
-        return (
-            grad.astype(bf16)
-            .reshape(n_dp, piece, n_tensor, columns)
-            .transpose(0, 2, 1, 3)
-        )
-
     def scatter(blocks):
-        flat = blocks.reshape((n_dp * n_tensor * blocks.shape[2],) + blocks.shape[3:])
-        return lax.psum_scatter(flat, groups, scatter_dimension=0, tiled=True).astype(f32)
+        flat = blocks.reshape((-1,) + blocks.shape[3:])
+        flat = flat.reshape(-1, width)
+        summed = lax.psum_scatter(flat, groups, scatter_dimension=0, tiled=True)
+        return summed.reshape(blocks.shape[2:]).astype(f32)
 
     grad_flow = cotangent.astype(f32)
     collected = [None] * layer_count
+    wide_slot = [None] * layer_count
+    narrow_slot = [None] * layer_count
+    slots = 3 * layer_count - 2
+    store, taken = None, 0
     for layer in reversed(range(layer_count)):
         (unit_one, scaled_one, normed_one, project, totals, mixed,
          unit_two, scaled_two, normed_two, active, slope) = kept[layer]
+        full_qkv, full_up, full_down, full_out = full[layer]
         branch_two = keep[layer, 1][:, None] * grad_flow
         grad_bias_down = jnp.sum(branch_two, axis=0)
         branch_two = branch_two.astype(bf16)
-        grad_down = by_block(dot_tokens(branch_two, active), hidden_cols)
-        grad_up = dot_rows(branch_two, full_down[layer]) * slope
+        grad_up = dot_rows(branch_two, full_down) * slope
         grad_bias_up = jnp.sum(grad_up, axis=0)
         grad_up = grad_up.astype(bf16)
-        grad_w_up = by_block(dot_tokens(normed_two, grad_up), hidden_cols)
-        wide = scatter(jnp.concatenate([grad_w_up, grad_down], axis=2))
+        wide = (normed_two, grad_up, branch_two, active)
+        if layer == layer_count - 1:
+            first = wide_gradients(*wide, (n_dp, n_tensor, 2, piece, width), None, 0)
+            grad_up, first = lax.optimization_barrier((grad_up, first))
+            first = scatter(first)
+        else:
+            wide_slot[layer] = taken
+            store = wide_gradients(*wide, (n_dp, n_tensor, slots, piece, width), store, taken)
+            taken += 2
+            grad_up, store = lax.optimization_barrier((grad_up, store))
         grad_part, grad_gain_two, grad_shift_two = norm_backward(
-            dot_rows(grad_up, full_up[layer]), unit_two, scaled_two, ln2_gain[layer]
+            jnp.dot(grad_up, full_up, preferred_element_type=f32),
+            unit_two, scaled_two, ln2_gain[layer],
         )
         grad_middle = grad_flow + grad_part
         branch_one = keep[layer, 0][:, None] * grad_middle
         grad_bias_out = jnp.sum(branch_one, axis=0)
         branch_one = branch_one.astype(bf16)
-        grad_out = by_block(dot_tokens(branch_one, mixed), head_cols)
-        grad_mixed = dot_rows(branch_one, full_out[layer]).astype(bf16)
+        grad_mixed = dot_rows(branch_one, full_out).astype(bf16)
         *grads, sums = attention_backward(project, feature_q, feature_k, grad_mixed, totals)
         grad_bias_qv = jnp.sum(sums, axis=0)[:2]
-        weights = full_qkv[layer].reshape(width, 3, width)
-        grad_one = sum(dot_rows(grads[part], weights[:, part]) for part in range(3))
-        narrow = [by_block(dot_tokens(normed_one, grad), head_cols) for grad in grads]
-        narrow = scatter(jnp.concatenate(narrow + [grad_out], axis=3))
+        if layer == 0:
+            first, *grads = lax.optimization_barrier((first, *grads))
+        narrow_slot[layer] = taken
+        store = narrow_gradients(
+            normed_one, grads, branch_one, mixed,
+            (n_dp, n_tensor, slots, piece, width), store, taken,
+        )
+        taken += 1
+        grads, store = lax.optimization_barrier((grads, store))
+        grad_one = sum(
+            jnp.dot(
+                grads[part],
+                full_qkv[part * width : (part + 1) * width],
+                preferred_element_type=f32,
+            )
+            for part in range(3)
+        )
         grad_part, grad_gain_one, grad_shift_one = norm_backward(
             grad_one, unit_one, scaled_one, ln1_gain[layer]
         )
         grad_flow = grad_middle + grad_part
-        collected[layer] = (
-            jnp.concatenate(
-                [grad_gain_one, grad_shift_one, grad_bias_qv.reshape(-1), grad_bias_out,
-                 grad_gain_two, grad_shift_two, grad_bias_down, grad_bias_up]
-            ),
-            narrow[:, : 3 * head_cols].reshape(piece, 3, head_cols),
-            narrow[:, 3 * head_cols :].T,
-            wide[:piece],
-            wide[piece:].T,
+        collected[layer] = jnp.concatenate(
+            [grad_gain_one, grad_shift_one, grad_bias_qv.reshape(-1), grad_bias_out,
+             grad_gain_two, grad_shift_two, grad_bias_down, grad_bias_up]
         )
-    small, grad_qkv, grad_out, grad_up, grad_down = [
-        jnp.stack([entry[position] for entry in collected]) for position in range(5)
+    small, later = lax.optimization_barrier((jnp.stack(collected), scatter(store)))
+    small = lax.psum(small, groups)
+    grad_qkv, grad_out, grad_up, grad_down = [], [], [], []
+    for layer in range(layer_count):
+        narrow = later[narrow_slot[layer]]
+        grad_qkv.append(narrow[:, : 3 * head_cols].reshape(piece, 3, head_cols))
+        grad_out.append(narrow[:, 3 * head_cols :].T)
+        wide = first if layer == layer_count - 1 else later[wide_slot[layer] :]
+        grad_up.append(wide[0])
+        grad_down.append(wide[1].T)
+    grad_qkv, grad_out, grad_up, grad_down = [
+        jnp.stack(parts) for parts in (grad_qkv, grad_out, grad_up, grad_down)
     ]
-    small = lax.psum(small, groups)
     gain_one, shift_one, query_bias, value_bias, bias_out, gain_two, shift_two, bias_down = [
         small[:, position * width : (position + 1) * width] for position in range(8)
     ]

time: 1260 us -> 859 us (0.68)
  local copies, waits for them, and re-layouts: 268 us -> 86.6 us
  waiting for transfers between devices: 575 us -> 432 us
  matrix products: 181 us -> 110 us
  Pallas kernels: 114 us -> 176 us
  other arithmetic: 80.7 us -> 31.3 us
  blocking collectives: 13.4 us -> 0 us
    reduce_scatter x4 -> x2, waiting for transfers between devices: 403 us -> 182 us  [scatter(): summed = lax.psum_scatter(flat, groups, scatter_dimension=0, tiled=True)]
    psum x1, waiting for transfers between devices: 0.01 us -> 123 us  [per_device(): small = lax.psum(small, groups)]
    reshape x25 -> x4, local copies, waits for them, and re-layouts: 106 us -> 1.68 us  [the longest x2 1.62 us: per_device(): bias_rows = jnp.concatenate([b_qv.reshape(-1), b_up.reshape(-1)])]
    dot_general x20 -> x12, matrix products: 117 us -> 49.3 us  [the longest x2 19.7 us: per_device(): jnp.dot(grad_up, full_up, preferred_element_type=f32)]
    pallas_call x0 -> x4, Pallas kernels: none -> 59.3 us  [blocked_gradients(): pl.pallas_call(kernel, grid=grid, in_specs=in_specs, out_specs=out_spec,...]
    concatenate x7 -> x2, other arithmetic: 46.5 us -> 0.8 us  [the longest x1 0.79 us: gather(): rows = jnp.concatenate(pieces, axis=0)]
    all_gather x4 -> x2, waiting for transfers between devices: 172 us -> 127 us  [gather(): gathered = lax.all_gather(rows, groups, axis=0, tiled=False)]
    concatenate x2 -> x1, local copies, waits for them, and re-layouts: 18.4 us -> 0.01 us  [gather(): rows = jnp.concatenate(pieces, axis=0)]
  transfers between devices with their start and end apart: 9 -> 5, of which waited for: 8 -> 4; matrix products, arithmetic and copies ran while one was open for 25% -> 14% of each run, Pallas kernels for 2% -> 15%
where the time goes in v2:
time: 859 us; the launch traced here: 852 us
  waiting for transfers between devices  432 us (50%)
  Pallas kernels  176 us (20%)
  matrix products  110 us (13%)
  local copies, waits for them, and re-layouts  86.6 us (10%)
  other arithmetic  31.3 us (4%)
  between operations  15.8 us (2%)
    reduce_scatter x2, waiting for transfers between devices, scatter(): summed = lax.psum_scatter(flat, groups, scatter_dimension=0, tiled=True)  182 us
    all_gather x2, waiting for transfers between devices, gather(): gathered = lax.all_gather(rows, groups, axis=0, tiled=False)  127 us
    psum x1, waiting for transfers between devices, per_device(): small = lax.psum(small, groups)  123 us
    pallas_call x2, Pallas kernels, attention_backward(): pl.pallas_call(attention_backward_kernel, grid=(tokens // SEQ, pairs), in...  73.7 us
    dot_general x8, matrix products, dot_rows(): lax.dot_general(left, right, (((1,), (1,)), ((), ())), preferred_element_...  60.9 us
    pallas_call x4, Pallas kernels, blocked_gradients(): pl.pallas_call(kernel, grid=grid, in_specs=in_specs, out_specs=out_spec,...  59.3 us
    pallas_call x2, Pallas kernels, attention_forward(): pl.pallas_call(attention_forward_kernel, grid=(tokens // SEQ, pairs), in_...  43 us
    transpose x12, local copies, waits for them, and re-layouts, rows_of(): rows.reshape(n_dp, n_tensor, parts, count, width).transpose(2, 1, 0, 3, 4)  32.8 us
  transfers between devices with their start and end apart: 5, of which 4 were waited for; matrix products, arithmetic and copies ran while one was open for 14% of the time, Pallas kernels for 15%

profile of v2, /device:TPU:8, one launch (start us, length us, event | category | flops | bytes accessed | tf_op | source)
XLA Modules:
  0.0 852.4 jit_solution(11884834079415733491)
XLA Ops:
  16.9 3.0 fusion.47
  25.2 103.1 %all-gather.5.cloned.1.call-done = bf16[9472,768]{1,0:T(8,128)(2,1)} async-done(((bf16[296,768]{1,0:T(8,128)(2,1)}), bf16[9472,768]{1,0:T(8,128)(2,1)}) %all-gather.5.cloned.1.call-update) | async-done | bytes 14549008 | tf_op jit(solution)/shard_map/all_gather | solution.py:333
  132.6 3.6 fusion.10
  139.1 4.1 slice.230
  144.7 7.2 slice_bitcast_fusion.2
  151.9 5.0 copy.78
  160.8 6.0 add_convert_fusion.1.q_ref.k_ref.v_ref
  166.8 21.4 %attend.2 = (bf16[1024,768]{1,0:T(8,128)(2,1)S(1)}, f32[1024,768]{1,0:T(8,128)S(1)}) custom-call(bf16[1024,2304]{1,0:T(8,128)(2,1)} %add_convert_fusion.1.q_ref.k_ref.v_ref, bf16[1024,2304]{1,0:T(8,128)(2,1)} %add_convert_fusion.1.q_ref.k_ref.v_ref, bf16[1024,2304]{1,0:T(8,128)(2,1)} %add_convert_fusion.1.q_ref.k_ref.v_ref, ...), custom_call_target="tpu_custom_call" | custom-call | flops 4831838208 | bytes 9437184 | tf_op jit(solution)/shard_map/attend/pallas_call | solution.py:133
  191.7 9.0 %multiply_convert_fusion.1 = (bf16[1024,3072]{1,0:T(8,128)(2,1)S(1)}, f32[1024,3072]{1,0:T(8,128)}) fusion(f32[3072]{0:T(1024)S(1)} %bitcast.218, bf16[1024,768]{1,0:T(8,128)(2,1)S(1)} %add_convert_fusion.5.norm_ref, bf16[3072,768]{1,0:T(8,128)(2,1)S(1)} %bitcast.177), kind=kOutput, calls=%fused_computation.14 | convolution fusion | flops 4850712576 | bytes 25178112 | tf_op jit(solution)/shard_map/dot_general | solution.py:52
  200.8 5.2 fusion.55
  208.2 24.4 %all-gather.7.cloned.1.call-done = bf16[9216,768]{1,0:T(8,128)(2,1)} async-done(((bf16[288,768]{1,0:T(8,128)(2,1)}), bf16[9216,768]{1,0:T(8,128)(2,1)}) %all-gather.7.cloned.1.call-update) | async-done | bytes 14155792 | tf_op jit(solution)/shard_map/all_gather | solution.py:333
  234.0 4.1 slice.296
  238.0 6.7 slice_bitcast_fusion
  244.9 5.0 copy.83
  253.5 5.5 add_convert_fusion.q_ref.k_ref.v_ref
  258.9 21.6 %attend.3 = (bf16[1024,768]{1,0:T(8,128)(2,1)S(1)}, f32[1024,768]{1,0:T(8,128)S(1)}) custom-call(bf16[1024,2304]{1,0:T(8,128)(2,1)} %add_convert_fusion.q_ref.k_ref.v_ref, bf16[1024,2304]{1,0:T(8,128)(2,1)} %add_convert_fusion.q_ref.k_ref.v_ref, bf16[1024,2304]{1,0:T(8,128)(2,1)} %add_convert_fusion.q_ref.k_ref.v_ref, ...), custom_call_target="tpu_custom_call" | custom-call | flops 4831838208 | bytes 9437184 | tf_op jit(solution)/shard_map/attend/pallas_call | solution.py:133
  283.8 10.7 %multiply_convert_fusion = (bf16[1024,3072]{1,0:T(8,128)(2,1)}, f32[1024,3072]{1,0:T(8,128)S(1)}) fusion(f32[3072]{0:T(1024)S(1)} %bitcast.220, bf16[1024,768]{1,0:T(8,128)(2,1)S(1)} %add_convert_fusion.3.norm_ref, bf16[3072,768]{1,0:T(8,128)(2,1)} %bitcast.184), kind=kOutput, calls=%fused_computation.12 | convolution fusion | flops 4850712576 | bytes 25178112 | tf_op jit(solution)/shard_map/dot_general | solution.py:52
  294.6 12.2 %fusion.46 = (f32[3072]{0:T(1024)S(1)}, bf16[1024,3072]{1,0:T(8,128)(2,1)}) fusion(f32[1024,3072]{1,0:T(8,128)S(1)} %get-tuple-element.229, f32[3072]{0:T(1024)S(1)} %bitcast.221, bf16[1024,768]{1,0:T(8,128)(2,1)S(1)} %copy-done.46, bf16[3072,768]{1,0:T(8,128)(2,1)S(1)} %bitcast.173), kind=kOutput, calls=%fused_computation.190 | convolution fusion | flops 4869583872 | bytes 25190400 | tf_op jit(solution)/shard_map/dot_general | solution.py:52
  306.8 17.9 %wide_grads.2 = bf16[8,4,2,96,768]{4,3,2,1,0:T(8,128)(2,1)} custom-call(bf16[1024,768]{1,0:T(8,128)(2,1)} %copy-done.47, bf16[1024,3072]{1,0:T(8,128)(2,1)} %get-tuple-element.56.up_ref, bf16[1024,768]{1,0:T(8,128)(2,1)} %get-tuple-element.194.branch_ref, bf16[1024,3072]{1,0:T(8,128)(2,1)} %get-tuple-element.228.active_ref), custom_call_target="tpu_custom_call" | custom-call | flops 9663676416 | bytes 22020096 | tf_op jit(solution)/shard_map/wide_grads/pallas_call | solution.py:221
  324.7 10.3 %multiply_reduce_fusion = (f32[768]{0:T(1024)S(1)}, f32[1024]{0:T(1024)S(1)}, f32[1024]{0:T(1024)S(1)}, f32[768]{0:T(1024)S(1)}, f32[1024,768]{1,0:T(8,128)}) fusion(f32[1024,768]{1,0:T(8,128)S(1)} %get-tuple-element.226, f32[1024]{0:T(1024)S(1)} %add_rsqrt_fusion, f32[1024]{0:T(1024)S(1)} %broadcast_multiply_fusion.9, f32[768]{0:T(1024)S(1)} %get-tuple-element.240, ...), kind=kOutput, calls=%fused_computation.44 | convolution fusion | flops 4838912000 | bytes 17327104 | tf_op jit(solution)/shard_map/dot_general | solution.py:451
  336.4 4.0 multiply_reduce_fusion.11
  343.3 36.9 %attend_back.2 = (bf16[1024,768]{1,0:T(8,128)(2,1)S(1)}, bf16[1024,768]{1,0:T(8,128)(2,1)S(1)}, bf16[1024,768]{1,0:T(8,128)(2,1)S(1)}, f32[1,8,768]{2,1,0:T(8,128)S(1)}) custom-call(bf16[1024,2304]{1,0:T(8,128)(2,1)} %add_convert_fusion.q_ref.k_ref.v_ref, bf16[1024,2304]{1,0:T(8,128)(2,1)} %add_convert_fusion.q_ref.k_ref.v_ref, ...), custom_call_target="tpu_custom_call" | custom-call | flops 12079595520 | bytes 14155776 | tf_op jit(solution)/shard_map/attend_back/pallas_call | solution.py:157
  383.6 12.0 %narrow_grads.2.rest_0_ = bf16[8,4,4,96,768]{4,3,2,1,0:T(8,128)(2,1)} custom-call(bf16[1024,768]{1,0:T(8,128)(2,1)} %copy-done.39, bf16[1024,768]{1,0:T(8,128)(2,1)} %copy-done.14, bf16[1024,768]{1,0:T(8,128)(2,1)} %copy-done.12, bf16[1024,768]{1,0:T(8,128)(2,1)} %copy-done.2, bf16[1024,768]{1,0:T(8,128)(2,1)} %copy-done.40, bf16[1024,768]{1,0:T(8,128)(2,1)} %copy-done.11), custom_call_target="tpu_custom_call" | custom-call | flops 4831838208 | bytes 11010048 | tf_op jit(solution)/shard_map/narrow_grads/pallas_call | solution.py:221
  395.6 2.8 fusion.35
  409.1 12.2 %fusion.45 = (f32[3072]{0:T(1024)S(1)}, bf16[1024,3072]{1,0:T(8,128)(2,1)}) fusion(f32[1024,3072]{1,0:T(8,128)S(1)} %bitcast.225, f32[3072]{0:T(1024)S(1)} %bitcast.219, bf16[1024,768]{1,0:T(8,128)(2,1)S(1)} %multiply_convert_fusion.3.branch_ref, bf16[3072,768]{1,0:T(8,128)(2,1)S(1)} %bitcast.183), kind=kOutput, calls=%fused_computation.189 | convolution fusion | flops 4869583872 | bytes 25190400 | tf_op jit(solution)/shard_map/dot_general | solution.py:52
  421.3 18.4 %wide_grads.3.rest_0_ = bf16[8,4,4,96,768]{4,3,2,1,0:T(8,128)(2,1)} custom-call(bf16[1024,768]{1,0:T(8,128)(2,1)} %copy-done.33, bf16[1024,3072]{1,0:T(8,128)(2,1)} %get-tuple-element.65.up_ref, bf16[1024,768]{1,0:T(8,128)(2,1)} %copy-done.35, bf16[1024,3072]{1,0:T(8,128)(2,1)} %copy-done.36, ...), custom_call_target="tpu_custom_call", output_to_operand_aliasing={{}: (4, {})} | custom-call | flops 9663676416 | bytes 22020096 | tf_op jit(solution)/shard_map/wide_grads/pallas_call | solution.py:221
  439.8 9.4 %multiply_reduce_fusion.2 = (f32[768]{0:T(1024)S(1)}, f32[1024]{0:T(1024)S(1)}, f32[1024]{0:T(1024)S(1)}, f32[768]{0:T(1024)S(1)}, f32[1024,768]{1,0:T(8,128)S(1)}) fusion(f32[1024,768]{1,0:T(8,128)S(1)} %copy-done.23, f32[1024]{0:T(1024)S(1)} %copy-done.63, f32[1024]{0:T(1024)S(1)} %copy-done.55, f32[768]{0:T(1024)S(1)} %copy-done.59, ...), kind=kOutput, calls=%fused_computation.46 | convolution fusion | flops 4838912000 | bytes 17327104 | tf_op jit(solution)/shard_map/dot_general | solution.py:451
  455.6 36.9 %attend_back.3 = (bf16[1024,768]{1,0:T(8,128)(2,1)S(1)}, bf16[1024,768]{1,0:T(8,128)(2,1)S(1)}, bf16[1024,768]{1,0:T(8,128)(2,1)S(1)}, f32[1,8,768]{2,1,0:T(8,128)S(1)}) custom-call(bf16[1024,2304]{1,0:T(8,128)(2,1)} %add_convert_fusion.1.q_ref.k_ref.v_ref, bf16[1024,2304]{1,0:T(8,128)(2,1)} %add_convert_fusion.1.q_ref.k_ref.v_ref, ...), custom_call_target="tpu_custom_call" | custom-call | flops 12079595520 | bytes 14155776 | tf_op jit(solution)/shard_map/attend_back/pallas_call | solution.py:157
  497.1 11.0 %narrow_grads.3 = bf16[8,4,4,96,768]{4,3,2,1,0:T(8,128)(2,1)} custom-call(bf16[1024,768]{1,0:T(8,128)(2,1)} %fusion.19.norm_ref, bf16[1024,768]{1,0:T(8,128)(2,1)} %copy-done.9, bf16[1024,768]{1,0:T(8,128)(2,1)} %copy-done.7, bf16[1024,768]{1,0:T(8,128)(2,1)} %copy-done.5, bf16[1024,768]{1,0:T(8,128)(2,1)} %copy-done.34, ...), custom_call_target="tpu_custom_call", output_to_operand_aliasing={{}: (6, {})} | custom-call | flops 4831838208 | bytes 11010048 | tf_op jit(solution)/shard_map/narrow_grads/pallas_call | solution.py:221
  508.9 9.5 %fusion.26 = bf16[1,1024,768]{2,1,0:T(8,128)(2,1)S(1)} fusion(f32[1024,768]{1,0:T(8,128)} %copy-done.21, f32[768]{0:T(1024)S(1)} %copy-done.75, bf16[1024,3072]{1,0:T(8,128)(2,1)} %get-tuple-element.228.active_ref, bf16[3072,768]{1,0:T(8,128)(2,1)} %bitcast.170, f32[1024]{0:T(1024)S(1)} %bitcast.217), kind=kOutput, calls=%fused_computation.79 | convolution fusion | flops 4834983936 | bytes 15735808 | tf_op jit(solution)/shard_map/dot_general | solution.py:409
  531.8 181.8 %reduce-scatter.5.cloned.1.call-done = bf16[384,768]{1,0:T(8,128)(2,1)} async-done(((bf16[12288,768]{1,0:T(8,128)(2,1)}), bf16[384,768]{1,0:T(8,128)(2,1)}) %reduce-scatter.5.cloned.1.call-update) | async-done | bytes 589840 | tf_op jit(solution)/shard_map/reduce_scatter | solution.py:421
  719.1 122.9 %all-reduce.3.cloned.1.call-done = f32[2,9216]{1,0:T(2,128)} async-done(((f32[2,9216]{1,0:T(2,128)}), f32[2,9216]{1,0:T(2,128)}) %all-reduce.3.cloned.1.call-update) | async-done | bytes 73744 | tf_op jit(solution)/shard_map/psum | solution.py:487
  (331 shorter events, 92.8 us)
Async XLA Ops:
  7.2 122.0 %copy-start = (s32[4,6]{1,0:T(4,128)S(1)}, s32[4,6]{1,0:T(4,128)}, u32[]{:S(2)}) copy-start(s32[4,6]{1,0:T(4,128)} %param.18) | copy-start | bytes 292
  7.2 121.1 %all-gather.5.cloned.1.call-start = ((), (), s32[]{:S(2)}) async-start(), calls=%async_computation.5 | async-start | bytes 15003648 | tf_op jit(solution)/shard_map/all_gather | solution.py:333
  16.8 113.4 %copy-start.69 = (bf16[2,768]{1,0:T(2,128)(2,1)S(1)}, bf16[2,768]{1,0:T(2,128)(2,1)}, u32[]{:S(2)}) copy-start(bf16[2,768]{1,0:T(2,128)(2,1)} %param.25) | copy-start | bytes 9220
  16.8 113.4 %copy-start.70 = (bf16[2,768]{1,0:T(2,128)(2,1)S(1)}, bf16[2,768]{1,0:T(2,128)(2,1)}, u32[]{:S(2)}) copy-start(bf16[2,768]{1,0:T(2,128)(2,1)} %param.31) | copy-start | bytes 9220
  16.8 114.0 %copy-start.71 = (f32[2,768]{1,0:T(2,128)S(1)}, f32[2,768]{1,0:T(2,128)}, u32[]{:S(2)}) copy-start(f32[2,768]{1,0:T(2,128)} %param.21) | copy-start | bytes 18436
  16.8 114.0 %copy-start.72 = (f32[2,768]{1,0:T(2,128)S(1)}, f32[2,768]{1,0:T(2,128)}, u32[]{:S(2)}) copy-start(f32[2,768]{1,0:T(2,128)} %param.20) | copy-start | bytes 18436
  16.8 114.0 %copy-start.73 = (f32[2,768]{1,0:T(2,128)S(1)}, f32[2,768]{1,0:T(2,128)}, u32[]{:S(2)}) copy-start(f32[2,768]{1,0:T(2,128)} %param.27) | copy-start | bytes 18436
  16.8 114.0 %copy-start.74 = (f32[2,768]{1,0:T(2,128)S(1)}, f32[2,768]{1,0:T(2,128)}, u32[]{:S(2)}) copy-start(f32[2,768]{1,0:T(2,128)} %param.26) | copy-start | bytes 18436
  16.9 114.3 %copy-start.28 = (bf16[1024,768]{1,0:T(8,128)(2,1)S(1)}, bf16[1024,768]{1,0:T(8,128)(2,1)}, u32[]{:S(2)}) copy-start(bf16[1024,768]{1,0:T(8,128)(2,1)} %param.16) | copy-start | bytes 4718596
  23.3 209.3 %all-gather.7.cloned.1.call-start = ((), (), s32[]{:S(2)}) async-start(), calls=%async_computation.6 | async-start | bytes 14598144 | tf_op jit(solution)/shard_map/all_gather | solution.py:333
  129.1 367.0 %reduce-scatter.3.cloned.1.call-start = ((), (), s32[]{:S(2)}) async-start(), calls=%async_computation.2 | async-start | bytes 9732096 | tf_op jit(solution)/shard_map/reduce_scatter | solution.py:421
  130.9 60.1 %copy-start.58 = (f32[768]{0:T(1024)}, f32[768]{0:T(1024)S(1)}, u32[]{:S(2)}) copy-start(f32[768]{0:T(1024)S(1)} %get-tuple-element.239) | copy-start | bytes 9220
  132.2 56.0 %copy-start.64 = (f32[1,1,1024]{2,1,0:T(1,128)}, f32[1,1,1024]{2,1,0:T(1,128)S(1)}, u32[]{:S(2)}) copy-start(f32[1,1,1024]{2,1,0:T(1,128)S(1)} %get-tuple-element.216) | copy-start | bytes 12292
  144.7 43.5 %copy-start.48 = (bf16[1,4,8,24,768]{4,3,2,1,0:T(8,128)(2,1)}, bf16[1,4,8,24,768]{4,3,2,1,0:T(8,128)(2,1)S(1)}, u32[]{:S(2)}) copy-start(bf16[1,4,8,24,768]{4,3,2,1,0:T(8,128)(2,1)S(1)} %copy.75) | copy-start | bytes 3538948
  166.8 24.9 %slice-start.2 = ((s8[4718592]{0:T(1024)(128)(4,1)}), s8[4194304]{0:T(1024)(128)(4,1)S(1)}, s32[]{:S(2)}) async-start(s8[4718592]{0:T(1024)(128)(4,1)} %bitcast.175), calls=%async_computation.9 | async-start | bytes 8388608
  190.5 10.3 %copy-start.22 = (f32[1024,768]{1,0:T(8,128)}, f32[1024,768]{1,0:T(8,128)S(1)}, u32[]{:S(2)}) copy-start(f32[1024,768]{1,0:T(8,128)S(1)} %get-tuple-element.220) | copy-start | bytes 9437188
  208.2 44.7 %copy-start.39 = (bf16[1024,768]{1,0:T(8,128)(2,1)}, bf16[1024,768]{1,0:T(8,128)(2,1)S(1)}, u32[]{:S(2)}) copy-start(bf16[1024,768]{1,0:T(8,128)(2,1)S(1)} %add_convert_fusion.4.norm_ref) | copy-start | bytes 4718596
  258.9 21.6 %copy-start.19 = (f32[1024,768]{1,0:T(8,128)S(1)}, f32[1024,768]{1,0:T(8,128)}, u32[]{:S(2)}) copy-start(f32[1024,768]{1,0:T(8,128)} %copy-done.18) | copy-start | bytes 9437188
  282.6 42.1 %copy-start.21 = (f32[1024,768]{1,0:T(8,128)}, f32[1024,768]{1,0:T(8,128)S(1)}, u32[]{:S(2)}) copy-start(f32[1024,768]{1,0:T(8,128)S(1)} %get-tuple-element.226) | copy-start | bytes 9437188
  283.2 11.3 %slice-start = ((s8[4718592]{0:T(1024)(128)(4,1)}), s8[4194304]{0:T(1024)(128)(4,1)S(1)}, s32[]{:S(2)}) async-start(s8[4718592]{0:T(1024)(128)(4,1)} %bitcast.171), calls=%async_computation.7 | async-start | bytes 8388608
  283.7 10.8 %copy-start.47 = (bf16[1024,768]{1,0:T(8,128)(2,1)}, bf16[1024,768]{1,0:T(8,128)(2,1)S(1)}, u32[]{:S(2)}) copy-start(bf16[1024,768]{1,0:T(8,128)(2,1)S(1)} %add_convert_fusion.3.norm_ref) | copy-start | bytes 4718596
  283.8 10.8 %slice-start.1 = ((s8[4718592]{0:T(1024)(128)(4,1)}), s8[524288]{0:T(1024)(128)(4,1)S(1)}, s32[]{:S(2)}) async-start(s8[4718592]{0:T(1024)(128)(4,1)} %bitcast.171), calls=%async_computation.8 | async-start | bytes 1048576
  283.8 10.8 %copy-start.46 = (bf16[1024,768]{1,0:T(8,128)(2,1)S(1)}, bf16[1024,768]{1,0:T(8,128)(2,1)}, u32[]{:S(2)}) copy-start(bf16[1024,768]{1,0:T(8,128)(2,1)} %get-tuple-element.194.branch_ref) | copy-start | bytes 4718596
  335.0 378.5 %reduce-scatter.5.cloned.1.call-start = ((), (), s32[]{:S(2)}) async-start(), calls=%async_computation.3 | async-start | bytes 19464192 | tf_op jit(solution)/shard_map/reduce_scatter | solution.py:421
  383.6 12.0 %copy-start.15 = (bf16[1024,768]{1,0:T(8,128)(2,1)S(1)}, bf16[1024,768]{1,0:T(8,128)(2,1)}, u32[]{:S(2)}) copy-start(bf16[1024,768]{1,0:T(8,128)(2,1)} %copy-done.14) | copy-start | bytes 4718596
  408.0 13.3 %copy-start.35 = (bf16[1024,768]{1,0:T(8,128)(2,1)}, bf16[1024,768]{1,0:T(8,128)(2,1)S(1)}, u32[]{:S(2)}) copy-start(bf16[1024,768]{1,0:T(8,128)(2,1)S(1)} %multiply_convert_fusion.3.branch_ref) | copy-start | bytes 4718596
  421.3 18.4 %copy-start.23 = (f32[1024,768]{1,0:T(8,128)S(1)}, f32[1024,768]{1,0:T(8,128)}, u32[]{:S(2)}) copy-start(f32[1024,768]{1,0:T(8,128)} %copy-done.22) | copy-start | bytes 9437188
  421.3 18.4 %copy-start.55 = (f32[1024]{0:T(1024)S(1)}, f32[1024]{0:T(1024)}, u32[]{:S(2)}) copy-start(f32[1024]{0:T(1024)} %copy-done.54) | copy-start | bytes 12292
  421.3 18.4 %copy-start.59 = (f32[768]{0:T(1024)S(1)}, f32[768]{0:T(1024)}, u32[]{:S(2)}) copy-start(f32[768]{0:T(1024)} %copy-done.58) | copy-start | bytes 9220
  421.3 18.4 %copy-start.63 = (f32[1024]{0:T(1024)S(1)}, f32[1024]{0:T(1024)}, u32[]{:S(2)}) copy-start(f32[1024]{0:T(1024)} %copy-done.62) | copy-start | bytes 12292
  508.2 333.8 %all-reduce.3.cloned.1.call-start = ((), (), s32[]{:S(2)}) async-start(), calls=%async_computation.4 | async-start | bytes 147456 | tf_op jit(solution)/shard_map/psum | solution.py:487
  715.1 130.2 %copy-start.1 = (s32[4,6]{1,0:T(4,128)S(1)}, s32[4,6]{1,0:T(4,128)}, u32[]{:S(2)}) copy-start(s32[4,6]{1,0:T(4,128)} %param.18) | copy-start | bytes 292
  (60 other events, 228.8 us)
Sparse Core Ops, SparseCore 0:
  23.4 104.7 all-gather.4
  131.6 100.9 all-gather.6
  335.2 134.6 reduce-scatter.2
  508.3 205.2 reduce-scatter.4
  719.0 122.8 all-reduce.2

commit v3 on v2

--- a/solution.py
+++ b/solution.py
@@ -171,6 +171,62 @@
     )(project, project, project, feature_q, feature_k, grad_mixed, totals)
 
 
+def unpack_kernel(got_ref, qkv_ref, up_ref, down_ref, out_ref):
+    blocks, hidden, few = up_ref.shape[1], up_ref.shape[2], out_ref.shape[2]
+    for block in range(blocks):
+        up_ref[0, block] = got_ref[block, 0, :hidden, :]
+        down_ref[0, block] = got_ref[block, 0, hidden : 2 * hidden, :]
+        out_ref[0, block] = got_ref[block, 0, 2 * hidden : 2 * hidden + few, :]
+        for part in range(3):
+            first = 2 * hidden + (1 + part) * few
+            qkv_ref[part, 0, block] = got_ref[block, 0, first : first + few, :]
+
+
+def unpack(got, hidden, few):
+    n_dp, n_tensor, rows, width = got.shape
+
+    def spec(count):
+        return pl.BlockSpec((1, n_dp, count, width), lambda t: (t, 0, 0, 0))
+
+    def shape(count):
+        return jax.ShapeDtypeStruct((n_tensor, n_dp, count, width), bf16)
+
+    outs = pl.pallas_call(
+        unpack_kernel,
+        grid=(n_tensor,),
+        in_specs=[pl.BlockSpec((n_dp, 1, rows, width), lambda t: (0, t, 0, 0))],
+        out_specs=[
+            pl.BlockSpec((3, 1, n_dp, few, width), lambda t: (0, t, 0, 0, 0)),
+            spec(hidden),
+            spec(hidden),
+            spec(few),
+        ],
+        out_shape=[
+            jax.ShapeDtypeStruct((3, n_tensor, n_dp, few, width), bf16),
+            shape(hidden),
+            shape(hidden),
+            shape(few),
+        ],
+        cost_estimate=pl.CostEstimate(
+            flops=0, bytes_accessed=4 * n_dp * n_tensor * rows * width, transcendentals=0
+        ),
+        compiler_params=pltpu.CompilerParams(vmem_limit_bytes=48 << 20),
+        name="unpack",
+    )(got)
+    return [array.reshape(-1, width) for array in outs]
+
+
+def sum_over(values, axis, size):
+    if size & (size - 1):
+        return lax.psum(values, axis)
+    reach = 1
+    while reach < size:
+        pairs = [(index, index ^ reach) for index in range(size)]
+        values = values + lax.ppermute(values, axis, pairs)
+        reach *= 2
+    return values
+
+
 def wide_kernel(norm_ref, up_ref, branch_ref, active_ref, *rest):
     out_ref, turned, result = rest[-3:]
     piece = out_ref.shape[3]
@@ -354,6 +410,8 @@
         return lax.optimization_barrier(rows.reshape(parts * n_dp * n_tensor * count, width))
 
     def weights_of(got):
+        if piece % 16 == 0 and hidden_piece == piece and out_piece % 8 == 0:
+            return unpack(got, hidden_piece, out_piece)
         up = rows_of(got, 0, hidden_piece)
         down = rows_of(got, hidden_piece, hidden_piece)
         out = rows_of(got, 2 * hidden_piece, out_piece)
@@ -483,8 +541,10 @@
             [grad_gain_one, grad_shift_one, grad_bias_qv.reshape(-1), grad_bias_out,
              grad_gain_two, grad_shift_two, grad_bias_down, grad_bias_up]
         )
-    small, later = lax.optimization_barrier((jnp.stack(collected), scatter(store)))
-    small = lax.psum(small, groups)
+    later = scatter(store)
+    small = jnp.stack(collected)
+    for axis in groups:
+        small = sum_over(small, axis, lax.axis_size(axis))
     grad_qkv, grad_out, grad_up, grad_down = [], [], [], []
     for layer in range(layer_count):
         narrow = later[narrow_slot[layer]]

time: 859 us -> 734 us (0.85)
  waiting for transfers between devices: 432 us -> 296 us
  local copies, waits for them, and re-layouts: 86.6 us -> 60.6 us
  Pallas kernels: 176 us -> 194 us
    psum x1 -> x0, waiting for transfers between devices: 123 us -> none  [per_device(): small = lax.psum(small, groups)]
    transpose x12 -> x0, local copies, waits for them, and re-layouts: 32.8 us -> none  [rows_of(): rows.reshape(n_dp, n_tensor, parts, count, width).transpose(2, 1, 0, 3, 4)]
    reduce_scatter x2, waiting for transfers between devices: 182 us -> 149 us  [scatter(): summed = lax.psum_scatter(flat, groups, scatter_dimension=0, tiled=True)]
    pallas_call x0 -> x2, Pallas kernels: none -> 18.2 us  [unpack(): pl.pallas_call(unpack_kernel, grid=(n_tensor,), in_specs=[pl.BlockSpec((n...]
    ppermute x0 -> x5, waiting for transfers between devices: none -> 11.2 us  [sum_over(): values = values + lax.ppermute(values, axis, pairs)]
    unnamed x198 -> x244, local copies, waits for them, and re-layouts: 26.8 us -> 36.9 us
  transfers between devices with their start and end apart: 5 -> 9, of which waited for: 4 -> 7; matrix products, arithmetic and copies ran while one was open for 14% -> 17% of each run, Pallas kernels for 15% -> 19%
where the time goes in v3:
time: 734 us; the launch traced here: 721 us
  waiting for transfers between devices  296 us (40%)
  Pallas kernels  194 us (26%)
  matrix products  114 us (16%)
  local copies, waits for them, and re-layouts  60.6 us (8%)
  other arithmetic  36.3 us (5%)
  between operations  15.4 us (2%)
    reduce_scatter x2, waiting for transfers between devices, scatter(): summed = lax.psum_scatter(flat, groups, scatter_dimension=0, tiled=True)  149 us
    all_gather x2, waiting for transfers between devices, gather(): gathered = lax.all_gather(rows, groups, axis=0, tiled=False)  135 us
    pallas_call x2, Pallas kernels, attention_backward(): pl.pallas_call(attention_backward_kernel, grid=(tokens // SEQ, pairs), in...  73.7 us
    dot_general x8, matrix products, dot_rows(): lax.dot_general(left, right, (((1,), (1,)), ((), ())), preferred_element_...  63.3 us
    pallas_call x4, Pallas kernels, blocked_gradients(): pl.pallas_call(kernel, grid=grid, in_specs=in_specs, out_specs=out_spec,...  58.9 us
    pallas_call x2, Pallas kernels, attention_forward(): pl.pallas_call(attention_forward_kernel, grid=(tokens // SEQ, pairs), in_...  42.8 us
    unnamed x244, local copies, waits for them, and re-layouts  36.9 us
    dot_general x2, matrix products, per_device(): jnp.dot(grad_up, full_up, preferred_element_type=f32)  20.9 us
  transfers between devices with their start and end apart: 9, of which 7 were waited for; matrix products, arithmetic and copies ran while one was open for 17% of the time, Pallas kernels for 19%

profile of v3, /device:TPU:8, one launch (start us, length us, event | category | flops | bytes accessed | tf_op | source)
XLA Modules:
  0.0 721.3 jit_solution(956698889036950498)
XLA Ops:
  10.8 2.8 fusion.42
  16.9 3.0 fusion.40
  25.2 103.1 %all-gather.5.cloned.1.call-done = bf16[9472,768]{1,0:T(8,128)(2,1)} async-done(((bf16[296,768]{1,0:T(8,128)(2,1)}), bf16[9472,768]{1,0:T(8,128)(2,1)}) %all-gather.5.cloned.1.call-update) | async-done | bytes 14549008 | tf_op jit(solution)/shard_map/all_gather | solution.py:389
  133.8 3.7 fusion.10
  140.4 9.0 %unpack.2 = (bf16[3,4,8,24,768]{4,3,2,1,0:T(8,128)(2,1)S(1)}, bf16[4,8,96,768]{3,2,1,0:T(8,128)(2,1)}, bf16[4,8,96,768]{3,2,1,0:T(8,128)(2,1)}, bf16[4,8,24,768]{3,2,1,0:T(8,128)(2,1)S(1)}) custom-call(bf16[8,4,296,768]{3,2,1,0:T(8,128)(2,1)} %bitcast.139), custom_call_target="tpu_custom_call" | custom-call | bytes 29097984 | tf_op jit(solution)/shard_map/unpack/pallas_call | solution.py:194
  151.2 5.5 add_convert_fusion.1.q_ref.k_ref.v_ref
  156.7 21.4 %attend.2 = (bf16[1024,768]{1,0:T(8,128)(2,1)S(1)}, f32[1024,768]{1,0:T(8,128)S(1)}) custom-call(bf16[1024,2304]{1,0:T(8,128)(2,1)} %add_convert_fusion.1.q_ref.k_ref.v_ref, bf16[1024,2304]{1,0:T(8,128)(2,1)} %add_convert_fusion.1.q_ref.k_ref.v_ref, bf16[1024,2304]{1,0:T(8,128)(2,1)} %add_convert_fusion.1.q_ref.k_ref.v_ref, ...), custom_call_target="tpu_custom_call" | custom-call | flops 4831838208 | bytes 9437184 | tf_op jit(solution)/shard_map/attend/pallas_call | solution.py:133
  182.5 9.3 %multiply_convert_fusion.1 = (bf16[1024,3072]{1,0:T(8,128)(2,1)S(1)}, f32[1024,3072]{1,0:T(8,128)}) fusion(f32[3072]{0:T(1024)S(1)} %bitcast.175, bf16[1024,768]{1,0:T(8,128)(2,1)S(1)} %add_convert_fusion.5.norm_ref, bf16[3072,768]{1,0:T(8,128)(2,1)S(1)} %bitcast.188), kind=kOutput, calls=%fused_computation.14 | convolution fusion | flops 4850712576 | bytes 25178112 | tf_op jit(solution)/shard_map/dot_general | solution.py:52
  191.9 5.2 fusion.49
  200.4 32.2 %all-gather.7.cloned.1.call-done = bf16[9216,768]{1,0:T(8,128)(2,1)} async-done(((bf16[288,768]{1,0:T(8,128)(2,1)}), bf16[9216,768]{1,0:T(8,128)(2,1)}) %all-gather.7.cloned.1.call-update) | async-done | bytes 14155792 | tf_op jit(solution)/shard_map/all_gather | solution.py:389
  232.7 9.1 %unpack.3 = (bf16[3,4,8,24,768]{4,3,2,1,0:T(8,128)(2,1)S(1)}, bf16[4,8,96,768]{3,2,1,0:T(8,128)(2,1)}, bf16[4,8,96,768]{3,2,1,0:T(8,128)(2,1)}, bf16[4,8,24,768]{3,2,1,0:T(8,128)(2,1)S(1)}) custom-call(bf16[8,4,288,768]{3,2,1,0:T(8,128)(2,1)} %bitcast.140), custom_call_target="tpu_custom_call" | custom-call | bytes 28311552 | tf_op jit(solution)/shard_map/unpack/pallas_call | solution.py:194
  241.8 5.6 add_convert_fusion.q_ref.k_ref.v_ref
  247.4 21.4 %attend.3 = (bf16[1024,768]{1,0:T(8,128)(2,1)S(1)}, f32[1024,768]{1,0:T(8,128)S(1)}) custom-call(bf16[1024,2304]{1,0:T(8,128)(2,1)} %add_convert_fusion.q_ref.k_ref.v_ref, bf16[1024,2304]{1,0:T(8,128)(2,1)} %add_convert_fusion.q_ref.k_ref.v_ref, bf16[1024,2304]{1,0:T(8,128)(2,1)} %add_convert_fusion.q_ref.k_ref.v_ref, bf16[1024,128]{1,0:T(8,128)(2,1)S(1)} %copy-done.19, ...), custom_call_target="tpu_custom_call" | custom-call | flops 4831838208 | bytes 9437184 | tf_op jit(solution)/shard_map/attend/pallas_call | solution.py:133
  272.3 10.7 %multiply_convert_fusion = (bf16[1024,3072]{1,0:T(8,128)(2,1)}, f32[1024,3072]{1,0:T(8,128)S(1)}) fusion(f32[3072]{0:T(1024)S(1)} %bitcast.177, bf16[1024,768]{1,0:T(8,128)(2,1)S(1)} %add_convert_fusion.3.norm_ref, bf16[3072,768]{1,0:T(8,128)(2,1)} %bitcast.195), kind=kOutput, calls=%fused_computation.12 | convolution fusion | flops 4850712576 | bytes 25178112 | tf_op jit(solution)/shard_map/dot_general | solution.py:52
  283.1 12.8 %fusion.37 = (f32[3072]{0:T(1024)}, bf16[1024,3072]{1,0:T(8,128)(2,1)}) fusion(f32[1024,3072]{1,0:T(8,128)S(1)} %get-tuple-element.245, f32[3072]{0:T(1024)S(1)} %bitcast.178, bf16[1024,768]{1,0:T(8,128)(2,1)S(1)} %copy-done.55, bf16[3072,768]{1,0:T(8,128)(2,1)S(1)} %bitcast.184), kind=kOutput, calls=%fused_computation.174 | convolution fusion | flops 4869583872 | bytes 25190400 | tf_op jit(solution)/shard_map/dot_general | solution.py:52
  295.9 17.9 %wide_grads.2 = bf16[8,4,2,96,768]{4,3,2,1,0:T(8,128)(2,1)} custom-call(bf16[1024,768]{1,0:T(8,128)(2,1)} %copy-done.56, bf16[1024,3072]{1,0:T(8,128)(2,1)} %get-tuple-element.70.up_ref, bf16[1024,768]{1,0:T(8,128)(2,1)} %get-tuple-element.208.branch_ref, bf16[1024,3072]{1,0:T(8,128)(2,1)} %get-tuple-element.244.active_ref), custom_call_target="tpu_custom_call" | custom-call | flops 9663676416 | bytes 22020096 | tf_op jit(solution)/shard_map/wide_grads/pallas_call | solution.py:277
  313.8 10.9 %multiply_reduce_fusion = (f32[768]{0:T(1024)}, f32[1024]{0:T(1024)}, f32[1024]{0:T(1024)}, f32[768]{0:T(1024)}, f32[1024,768]{1,0:T(8,128)}) fusion(f32[1024,768]{1,0:T(8,128)S(1)} %get-tuple-element.242, f32[1024]{0:T(1024)S(1)} %add_rsqrt_fusion, f32[1024]{0:T(1024)S(1)} %broadcast_multiply_fusion.9, f32[768]{0:T(1024)S(1)} %copy-done.78, ...), kind=kOutput, calls=%fused_computation.40 | convolution fusion | flops 4838912000 | bytes 17327104 | tf_op jit(solution)/shard_map/dot_general | solution.py:509
  326.2 4.7 multiply_reduce_fusion.11
  335.7 36.9 %attend_back.2 = (bf16[1024,768]{1,0:T(8,128)(2,1)S(1)}, bf16[1024,768]{1,0:T(8,128)(2,1)S(1)}, bf16[1024,768]{1,0:T(8,128)(2,1)S(1)}, f32[1,8,768]{2,1,0:T(8,128)S(1)}) custom-call(bf16[1024,2304]{1,0:T(8,128)(2,1)} %add_convert_fusion.q_ref.k_ref.v_ref, bf16[1024,2304]{1,0:T(8,128)(2,1)} %add_convert_fusion.q_ref.k_ref.v_ref, ...), custom_call_target="tpu_custom_call" | custom-call | flops 12079595520 | bytes 14155776 | tf_op jit(solution)/shard_map/attend_back/pallas_call | solution.py:157
  376.8 11.0 %narrow_grads.2.rest_0_ = bf16[8,4,4,96,768]{4,3,2,1,0:T(8,128)(2,1)} custom-call(bf16[1024,768]{1,0:T(8,128)(2,1)} %add_convert_fusion.4.norm_ref, bf16[1024,768]{1,0:T(8,128)(2,1)} %copy-done.16, bf16[1024,768]{1,0:T(8,128)(2,1)} %copy-done.14, bf16[1024,768]{1,0:T(8,128)(2,1)} %copy-done.2, bf16[1024,768]{1,0:T(8,128)(2,1)} %copy-done.50, ...), custom_call_target="tpu_custom_call" | custom-call | flops 4831838208 | bytes 11010048 | tf_op jit(solution)/shard_map/narrow_grads/pallas_call | solution.py:277
  393.2 3.1 multiply_reduce_fusion.1
  396.3 2.7 multiply_reduce_fusion.10
  399.8 14.3 %fusion.36 = (f32[3072]{0:T(1024)}, bf16[1024,3072]{1,0:T(8,128)(2,1)}) fusion(f32[1024,3072]{1,0:T(8,128)} %get-tuple-element.238, f32[3072]{0:T(1024)S(1)} %bitcast.176, bf16[1024,768]{1,0:T(8,128)(2,1)S(1)} %multiply_convert_fusion.3.branch_ref, bf16[3072,768]{1,0:T(8,128)(2,1)S(1)} %bitcast.194), kind=kOutput, calls=%fused_computation.173 | convolution fusion | flops 4869583872 | bytes 25190400 | tf_op jit(solution)/shard_map/dot_general | solution.py:52
  414.1 18.9 %wide_grads.3.rest_0_ = bf16[8,4,4,96,768]{4,3,2,1,0:T(8,128)(2,1)} custom-call(bf16[1024,768]{1,0:T(8,128)(2,1)} %copy-done.45, bf16[1024,3072]{1,0:T(8,128)(2,1)} %get-tuple-element.79.up_ref, bf16[1024,768]{1,0:T(8,128)(2,1)} %copy-done.47, bf16[1024,3072]{1,0:T(8,128)(2,1)} %copy-done.48, ...), custom_call_target="tpu_custom_call", output_to_operand_aliasing={{}: (4, {})} | custom-call | flops 9663676416 | bytes 22020096 | tf_op jit(solution)/shard_map/wide_grads/pallas_call | solution.py:277
  433.0 10.0 %multiply_reduce_fusion.2 = (f32[768]{0:T(1024)}, f32[1024]{0:T(1024)S(1)}, f32[1024]{0:T(1024)S(1)}, f32[768]{0:T(1024)}, f32[1024,768]{1,0:T(8,128)S(1)}) fusion(f32[1024,768]{1,0:T(8,128)S(1)} %copy-done.37, f32[1024]{0:T(1024)S(1)} %copy-done.75, f32[1024]{0:T(1024)S(1)} %copy-done.67, f32[768]{0:T(1024)S(1)} %copy-done.71, ...), kind=kOutput, calls=%fused_computation.42 | convolution fusion | flops 4838912000 | bytes 17327104 | tf_op jit(solution)/shard_map/dot_general | solution.py:509
  449.3 36.8 %attend_back.3 = (bf16[1024,768]{1,0:T(8,128)(2,1)S(1)}, bf16[1024,768]{1,0:T(8,128)(2,1)S(1)}, bf16[1024,768]{1,0:T(8,128)(2,1)S(1)}, f32[1,8,768]{2,1,0:T(8,128)S(1)}) custom-call(bf16[1024,2304]{1,0:T(8,128)(2,1)} %add_convert_fusion.1.q_ref.k_ref.v_ref, bf16[1024,2304]{1,0:T(8,128)(2,1)} %add_convert_fusion.1.q_ref.k_ref.v_ref, ...), custom_call_target="tpu_custom_call" | custom-call | flops 12079595520 | bytes 14155776 | tf_op jit(solution)/shard_map/attend_back/pallas_call | solution.py:157
  492.0 11.1 %narrow_grads.3 = bf16[8,4,4,96,768]{4,3,2,1,0:T(8,128)(2,1)} custom-call(bf16[1024,768]{1,0:T(8,128)(2,1)} %fusion.19.norm_ref, bf16[1024,768]{1,0:T(8,128)(2,1)} %copy-done.11, bf16[1024,768]{1,0:T(8,128)(2,1)} %copy-done.9, bf16[1024,768]{1,0:T(8,128)(2,1)} %copy-done.7, bf16[1024,768]{1,0:T(8,128)(2,1)} %copy-done.46, ...), custom_call_target="tpu_custom_call", output_to_operand_aliasing={{}: (6, {})} | custom-call | flops 4831838208 | bytes 11010048 | tf_op jit(solution)/shard_map/narrow_grads/pallas_call | solution.py:277
  518.9 10.3 %fusion.26 = bf16[1,1024,768]{2,1,0:T(8,128)(2,1)S(1)} fusion(f32[1024,768]{1,0:T(8,128)} %copy-done.35, f32[768]{0:T(1024)} %get-tuple-element.180, bf16[1024,3072]{1,0:T(8,128)(2,1)} %get-tuple-element.244.active_ref, bf16[3072,768]{1,0:T(8,128)(2,1)} %bitcast.181, f32[1024]{0:T(1024)} %bitcast.174), kind=kOutput, calls=%fused_computation.75 | convolution fusion | flops 4834983936 | bytes 15735808 | tf_op jit(solution)/shard_map/dot_general | solution.py:467
  540.3 3.2 collective-permute-done.1
  545.0 3.0 collective-permute-done.2
  554.1 3.7 collective-permute-done.4
  559.7 149.4 %reduce-scatter.5.cloned.1.call-done = bf16[384,768]{1,0:T(8,128)(2,1)} async-done(((bf16[12288,768]{1,0:T(8,128)(2,1)}), bf16[384,768]{1,0:T(8,128)(2,1)}) %reduce-scatter.5.cloned.1.call-update) | async-done | bytes 589840 | tf_op jit(solution)/shard_map/reduce_scatter | solution.py:479
  (376 shorter events, 103.3 us)
Async XLA Ops:
  7.2 122.0 %copy-start = (s32[4,6]{1,0:T(4,128)S(1)}, s32[4,6]{1,0:T(4,128)}, u32[]{:S(2)}) copy-start(s32[4,6]{1,0:T(4,128)} %param.18) | copy-start | bytes 292
  7.2 121.1 %all-gather.5.cloned.1.call-start = ((), (), s32[]{:S(2)}) async-start(), calls=%async_computation.4 | async-start | bytes 15003648 | tf_op jit(solution)/shard_map/all_gather | solution.py:389
  16.8 113.4 %copy-start.88 = (bf16[2,768]{1,0:T(2,128)(2,1)S(1)}, bf16[2,768]{1,0:T(2,128)(2,1)}, u32[]{:S(2)}) copy-start(bf16[2,768]{1,0:T(2,128)(2,1)} %param.25) | copy-start | bytes 9220
  16.8 114.0 %copy-start.89 = (bf16[2,768]{1,0:T(2,128)(2,1)S(1)}, bf16[2,768]{1,0:T(2,128)(2,1)}, u32[]{:S(2)}) copy-start(bf16[2,768]{1,0:T(2,128)(2,1)} %param.31) | copy-start | bytes 9220
  16.8 114.6 %copy-start.95 = (f32[2,768]{1,0:T(2,128)S(1)}, f32[2,768]{1,0:T(2,128)}, u32[]{:S(2)}) copy-start(f32[2,768]{1,0:T(2,128)} %param.21) | copy-start | bytes 18436
  16.8 114.6 %copy-start.96 = (f32[2,768]{1,0:T(2,128)S(1)}, f32[2,768]{1,0:T(2,128)}, u32[]{:S(2)}) copy-start(f32[2,768]{1,0:T(2,128)} %param.20) | copy-start | bytes 18436
  16.8 114.6 %copy-start.97 = (f32[2,768]{1,0:T(2,128)S(1)}, f32[2,768]{1,0:T(2,128)}, u32[]{:S(2)}) copy-start(f32[2,768]{1,0:T(2,128)} %param.27) | copy-start | bytes 18436
  16.8 114.6 %copy-start.98 = (f32[2,768]{1,0:T(2,128)S(1)}, f32[2,768]{1,0:T(2,128)}, u32[]{:S(2)}) copy-start(f32[2,768]{1,0:T(2,128)} %param.26) | copy-start | bytes 18436
  16.9 115.5 %copy-start.42 = (bf16[1024,768]{1,0:T(8,128)(2,1)S(1)}, bf16[1024,768]{1,0:T(8,128)(2,1)}, u32[]{:S(2)}) copy-start(bf16[1024,768]{1,0:T(8,128)(2,1)} %param.16) | copy-start | bytes 4718596
  23.3 209.4 %all-gather.7.cloned.1.call-start = ((), (), s32[]{:S(2)}) async-start(), calls=%async_computation.5 | async-start | bytes 14598144 | tf_op jit(solution)/shard_map/all_gather | solution.py:389
  129.1 361.1 %reduce-scatter.3.cloned.1.call-start = ((), (), s32[]{:S(2)}) async-start(), calls=%async_computation.2 | async-start | bytes 9732096 | tf_op jit(solution)/shard_map/reduce_scatter | solution.py:479
  132.1 49.8 %copy-start.70 = (f32[768]{0:T(1024)}, f32[768]{0:T(1024)S(1)}, u32[]{:S(2)}) copy-start(f32[768]{0:T(1024)S(1)} %get-tuple-element.255) | copy-start | bytes 9220
  133.3 44.8 %copy-start.76 = (f32[1,1,1024]{2,1,0:T(1,128)}, f32[1,1,1024]{2,1,0:T(1,128)S(1)}, u32[]{:S(2)}) copy-start(f32[1,1,1024]{2,1,0:T(1,128)S(1)} %get-tuple-element.232) | copy-start | bytes 12292
  133.3 58.5 %copy-start.80 = (f32[1,1,1024]{2,1,0:T(1,128)}, f32[1,1,1024]{2,1,0:T(1,128)S(1)}, u32[]{:S(2)}) copy-start(f32[1,1,1024]{2,1,0:T(1,128)S(1)} %get-tuple-element.231) | copy-start | bytes 12292
  133.3 135.5 %copy-start.82 = (f32[1,1,1024]{2,1,0:T(1,128)}, f32[1,1,1024]{2,1,0:T(1,128)S(1)}, u32[]{:S(2)}) copy-start(f32[1,1,1024]{2,1,0:T(1,128)S(1)} %get-tuple-element.230) | copy-start | bytes 12292
  133.6 23.1 %copy-start.18 = (bf16[1024,128]{1,0:T(8,128)(2,1)}, bf16[1024,128]{1,0:T(8,128)(2,1)S(1)}, u32[]{:S(2)}) copy-start(bf16[1024,128]{1,0:T(8,128)(2,1)S(1)} %compare_convert_fusion.fq_ref) | copy-start | bytes 786436
  133.8 22.9 %copy-start.21 = (bf16[1024,128]{1,0:T(8,128)(2,1)}, bf16[1024,128]{1,0:T(8,128)(2,1)S(1)}, u32[]{:S(2)}) copy-start(bf16[1024,128]{1,0:T(8,128)(2,1)S(1)} %select_convert_fusion.fk_ref) | copy-start | bytes 786436
  149.4 28.7 %copy-start.26 = (bf16[4,8,24,768]{3,2,1,0:T(8,128)(2,1)}, bf16[4,8,24,768]{3,2,1,0:T(8,128)(2,1)S(1)}, u32[]{:S(2)}) copy-start(bf16[4,8,24,768]{3,2,1,0:T(8,128)(2,1)S(1)} %get-tuple-element.58) | copy-start | bytes 3538948
  156.7 25.8 %slice-start.2 = ((s8[4718592]{0:T(1024)(128)(4,1)}), s8[4194304]{0:T(1024)(128)(4,1)S(1)}, s32[]{:S(2)}) async-start(s8[4718592]{0:T(1024)(128)(4,1)} %bitcast.186), calls=%async_computation.8 | async-start | bytes 8388608
  241.8 27.1 %copy-start.28 = (bf16[4,8,24,768]{3,2,1,0:T(8,128)(2,1)}, bf16[4,8,24,768]{3,2,1,0:T(8,128)(2,1)S(1)}, u32[]{:S(2)}) copy-start(bf16[4,8,24,768]{3,2,1,0:T(8,128)(2,1)S(1)} %get-tuple-element.67) | copy-start | bytes 3538948
  247.4 21.5 %copy-start.33 = (f32[1024,768]{1,0:T(8,128)S(1)}, f32[1024,768]{1,0:T(8,128)}, u32[]{:S(2)}) copy-start(f32[1024,768]{1,0:T(8,128)} %copy-done.32) | copy-start | bytes 9437188
  247.4 21.5 %copy-start.99 = (f32[768]{0:T(1024)S(1)}, f32[768]{0:T(1024)}, u32[]{:S(2)}) copy-start(f32[768]{0:T(1024)} %get-tuple-element.182) | copy-start | bytes 9220
  271.0 42.8 %copy-start.35 = (f32[1024,768]{1,0:T(8,128)}, f32[1024,768]{1,0:T(8,128)S(1)}, u32[]{:S(2)}) copy-start(f32[1024,768]{1,0:T(8,128)S(1)} %get-tuple-element.242) | copy-start | bytes 9437188
  271.5 42.3 %copy-start.79 = (f32[1024]{0:T(1024)}, f32[1024]{0:T(1024)S(1)}, u32[]{:S(2)}) copy-start(f32[1024]{0:T(1024)S(1)} %add_rsqrt_fusion) | copy-start | bytes 12292
  324.7 384.4 %reduce-scatter.5.cloned.1.call-start = ((), (), s32[]{:S(2)}) async-start(), calls=%async_computation.3 | async-start | bytes 19464192 | tf_op jit(solution)/shard_map/reduce_scatter | solution.py:479
  414.1 18.9 %copy-start.71 = (f32[768]{0:T(1024)S(1)}, f32[768]{0:T(1024)}, u32[]{:S(2)}) copy-start(f32[768]{0:T(1024)} %copy-done.70) | copy-start | bytes 9220
  414.1 18.9 %copy-start.75 = (f32[1024]{0:T(1024)S(1)}, f32[1024]{0:T(1024)}, u32[]{:S(2)}) copy-start(f32[1024]{0:T(1024)} %copy-done.74) | copy-start | bytes 12292
  536.6 2.1 collective-permute-start
  538.8 4.6 collective-permute-start.1
  543.6 4.4 collective-permute-start.2
  548.0 4.4 collective-permute-start.3
  552.5 5.3 collective-permute-start.4
  (87 other events, 428.3 us)
Sparse Core Ops, SparseCore 0:
  23.4 104.7 all-gather.4
  131.6 100.9 all-gather.6
  324.9 134.6 reduce-scatter.2
  503.2 205.8 reduce-scatter.4
